TPU v7x, 32 devices: a whole 2x2x4 slice. The times are simulated.
32 devices in a mesh: slab: 16 (over z, y, x), feat: 2 (over core).
Axes of the slice: x: 2, y: 2, z: 4, core: 2. Of those that a mesh axis runs over, the one named last changes fastest.
Arguments:
- states: float32 [40, 8192], P(None, ('slab', 'feat')), may hold values from -6 to 6
- inputs: float32 [8192], P(('slab', 'feat')), may hold values from -4 to 4
- targets: float32 [40, 8192], P(None, ('slab', 'feat')), may hold values from -4 to 4
Outputs:
- local_operators: float32 [16, 40, 862], P('slab', 'feat')
- scaled_duals: float32 [16, 40, 862], P('slab', 'feat')
- consensus: float32 [40, 862], P('feat')
- residual_history: float32 [2, 2], replicated
All inputs are finite; a program needn't handle non-finite values.
Results may differ from a plain program's by a relative error of at most 0.0003.
Values sent between devices are 32-bit elements; how exact they have to be, the bound alone decides.
A program may use at most 64 MiB of HBM per device.

v0:
```python
import functools

import jax
import jax.numpy as jnp
from jax import lax
from jax.experimental import pallas as pl
from jax.experimental.pallas import tpu as pltpu
from jax.sharding import PartitionSpec as P

penalty = 1.0
NN = (((1,), (0,)), ((), ()))
NT = (((1,), (1,)), ((), ()))


def exact(left, right, dims=NN):
    return lax.dot_general(left, right, dims, precision=lax.Precision.HIGHEST, preferred_element_type=jnp.float32)


def fast(left, right, dims=NN):
    return lax.dot_general(
        left.astype(jnp.bfloat16), right.astype(jnp.bfloat16), dims, preferred_element_type=jnp.float32
    )


def split(value):
    high = value.astype(jnp.bfloat16)
    return high, (value - high.astype(jnp.float32)).astype(jnp.bfloat16)


def triple(left, right):
    lh, ll = split(left)
    rh, rl = split(right)
    return fast(lh, rh) + (fast(lh, rl) + fast(ll, rh))


def eye_mask(size):
    return lax.broadcasted_iota(jnp.int32, (size, size), 0) == lax.broadcasted_iota(jnp.int32, (size, size), 1)


def refined_solve(right_side, system, inverse):
    answer = fast(right_side, inverse)
    for multiply in (triple, triple, exact):
        answer = answer + fast(right_side - multiply(answer, system), inverse)
    return answer


def invert_by_pivots(source, target):
    size = source.shape[0]
    target[...] = source[...]
    sub = lax.broadcasted_iota(jnp.int32, (size, 1), 0)
    lane = lax.broadcasted_iota(jnp.int32, (1, size), 1)

    def step(k, carry):
        row = target[pl.ds(k, 1), :]
        here = lane == k
        pivot = jnp.sum(jnp.where(here, row, 0.0), axis=1, keepdims=True)
        scaled = jnp.where(here, 1.0, row) / pivot
        whole = target[...]
        column = jnp.sum(jnp.where(here, whole, 0.0), axis=1, keepdims=True)
        column = jnp.where(sub == k, -1.0, column)
        kept = jnp.where(here | (sub == k), 0.0, whole)
        target[...] = kept - column * scaled
        return carry

    lax.fori_loop(0, size, step, 0)


def build_features(packed, phi, wanted, reduced, feats):
    count = packed.shape[1]
    half = reduced // feats
    row = reduced
    phi[0:reduced, :] = packed[0:reduced, :]
    for i in range(reduced):
        phi[row : row + reduced - i, :] = packed[i : i + 1, :] * packed[i:reduced, :]
        row += reduced - i
    phi[row : row + 1, :] = packed[2 * reduced : 2 * reduced + 1, :]
    phi[row + 1 : row + 2, :] = jnp.ones((1, count), jnp.float32)
    if row + 2 < phi.shape[0]:
        phi[row + 2 :, :] = jnp.zeros((phi.shape[0] - row - 2, count), jnp.float32)
    wanted[...] = jnp.zeros(wanted.shape, jnp.float32)
    me = lax.axis_index("feat")
    for f in range(feats):

        @pl.when(me == f)
        def _():
            wanted[0:half, :] = packed[reduced + f * half : reduced + (f + 1) * half, :]


def first_kernel(packed, system, inverse, shifted, *, reduced):
    count = packed.shape[1]
    signal = packed[2 * reduced : 2 * reduced + 1, :]
    s = packed[0:reduced, :]
    extra = jnp.concatenate([s * s * (0.5**0.5), jnp.broadcast_to(signal, (8, count)) * (8.0**-0.5)], 0)
    inner = exact(s.T, s)
    diagonal = eye_mask(count)
    a = (inner + 0.5 * inner * inner + exact(extra.T, extra) + 1.0) * (1.0 / count)
    a = a + jnp.where(diagonal, penalty, 0.0)
    system[...] = a

    high = jnp.max(jnp.sum(jnp.abs(a), axis=0, keepdims=True)) / penalty
    delta = (high - 1.0) / (high + 1.0)
    alpha = 2.0 / ((1.0 + high) * penalty)
    c = 2.0 / (2.0 - delta * delta)
    inverse[...] = (c * alpha) * (jnp.where(diagonal, 2.0, 0.0) - alpha * a)
    delta = delta * delta / (2.0 - delta * delta)

    def coarse(state):
        step, delta = state
        x = inverse[...].astype(jnp.bfloat16)
        shifted[...] = fast(system[...], x)
        c = 2.0 / (2.0 - delta * delta)
        inverse[...] = c * (2.0 * inverse[...] - fast(x, shifted[...]))
        return step + 1, delta * delta / (2.0 - delta * delta)

    lax.while_loop(lambda state: (state[1] > 0.1) & (state[0] < 12), coarse, (0, delta))

    def polish(state):
        step, _ = state
        x = inverse[...]
        gap = jnp.where(eye_mask(count), 1.0, 0.0) - triple(system[...], x)
        shifted[...] = gap
        worst = jnp.sum(jnp.sum(gap * gap, axis=0, keepdims=True))
        inverse[...] = inverse[...] + fast(inverse[...], shifted[...])
        return step + 1, worst

    _, worst = lax.while_loop(
        lambda state: jnp.logical_not(state[1] < 0.02) & (state[0] < 6), polish, (0, jnp.float32(1e9))
    )

    @pl.when(jnp.logical_not(worst < 0.02))
    def _():
        invert_by_pivots(system, inverse)


def to_tiles(value, tiles):
    rows, columns = value.shape
    spot = 0
    for c in range(0, columns, 128):
        for r in range(0, rows, 8):
            tiles[spot] = value[r : r + 8, c : c + 128]
            spot += 1
    for rest in range(spot, tiles.shape[0]):
        tiles[rest] = jnp.zeros((8, 128), jnp.float32)


def from_tiles(tile, rows, columns):
    high = rows // 8
    strips = []
    for c in range(columns // 128):
        strips.append(jnp.concatenate([tile(c * high + r) for r in range(high)], 0))
    return jnp.concatenate(strips, 1)


def total(value):
    flat = value.reshape(-1, 8, 128).sum(0)
    return jnp.sum(jnp.sum(flat, axis=1, keepdims=True), axis=0, keepdims=True)


def second_kernel(
    packed, system, inverse, after, duals, last, history,
    local, tiles, phi, wanted, better, received, gathered, received2, gathered2, foreign, tiles2, stats,
    scatter_send, scatter_recv, gather_send, gather_recv,
    scatter_send2, scatter_recv2, gather_send2, gather_recv2, foreign_send, foreign_recv,
    *, reduced, width,
):
    slabs = lax.axis_size("slab")
    feats = lax.axis_size("feat")
    me = lax.axis_index("slab")
    core = lax.axis_index("feat")
    owners, extended = gathered2.shape[0], gathered2.shape[1]
    chunk = extended - 1
    rows, columns = local.shape

    def peer(d):
        return lax.rem(me + d, slabs)

    def feat_of(f):
        return lax.rem(core + f, feats)

    def copy(source, target, send, recv, slab, feat):
        return pltpu.make_async_remote_copy(
            src_ref=source, dst_ref=target, send_sem=send, recv_sem=recv,
            device_id={"slab": slab, "feat": feat}, device_id_type=pl.DeviceIdType.MESH,
        )

    def each(first, stop, body):
        if stop - first <= 16:
            for d in range(first, stop):
                body(d)
            return

        def step(d, carry):
            body(d)
            return carry

        lax.fori_loop(first, stop, step, 0)

    barrier = pltpu.get_barrier_semaphore()
    for f in range(feats):

        def greet(d, f=f):
            pl.semaphore_signal(
                barrier, inc=1, device_id={"slab": peer(d), "feat": feat_of(f)},
                device_id_type=pl.DeviceIdType.MESH,
            )

        each(1 if f == 0 else 0, slabs, greet)
    build_features(packed, phi, wanted, reduced, feats)
    y = refined_solve(wanted[...] * (1.0 / phi.shape[1]), system[...], inverse[...])
    start_value = exact(y, phi[...], NT)
    local[...] = start_value
    to_tiles(start_value, tiles)
    pl.semaphore_wait(barrier, slabs * feats - 1)

    def scatter(source, landing, send, recv):
        def piece(d):
            owner = peer(d)
            return copy(source.at[pl.ds(owner * chunk, chunk)], landing.at[d], send.at[d], recv.at[d], owner, core)

        def start(d):
            @pl.when(peer(d) < owners)
            def _():
                piece(d).start()

        def finish(d):
            @pl.when(peer(d) < owners)
            def _():
                piece(d).wait_send()

        each(1, slabs, start)
        return finish

    def arrivals(source, landing, send, recv):
        def wait(d):
            copy(source.at[pl.ds(0, chunk)], landing.at[d], send.at[d], recv.at[d], me, core).wait_recv()

        each(1, slabs, wait)

    def spread(buffer, send, recv):
        def piece(d):
            return copy(buffer.at[me], buffer.at[me], send.at[d], recv.at[me], peer(d), core)

        each(1, slabs, lambda d: piece(d).start())
        return lambda d: piece(d).wait_send()

    def collected(buffer, send, recv):
        def wait(o):
            @pl.when(o != me)
            def _():
                copy(buffer.at[o], buffer.at[o], send.at[0], recv.at[o], me, core).wait_recv()

        each(0, owners, wait)

    def polished(x):
        gap = jnp.where(eye_mask(x.shape[0]), 1.0, 0.0) - exact(system[...], x)
        return x + fast(x, gap)

    end1 = scatter(tiles, received, scatter_send, scatter_recv)
    better[...] = polished(inverse[...])

    @pl.when(me < owners)
    def _():
        arrivals(tiles, received, scatter_send, scatter_recv)
        mine = tiles[pl.ds(me * chunk, chunk)]
        others = received[1:slabs]
        mean = (mine + others.sum(0)) * (1.0 / slabs)
        gathered[me] = mean
        spread(gathered, gather_send, gather_recv)
        primal = total(jnp.square(mine - mean)) + total(jnp.square(others - mean[None]))
        stats[0] = jnp.broadcast_to(primal, (8, 128))
        stats[1] = jnp.broadcast_to((slabs * penalty * penalty) * total(jnp.square(mean)), (8, 128))

    better[...] = polished(better[...])
    collected(gathered, gather_send, gather_recv)
    mean = from_tiles(lambda t: gathered[t // chunk, t % chunk], rows, columns)
    first = local[...]
    c = 2.0 * mean - first
    z = exact(c, phi[...]) * (1.0 / (phi.shape[1] * penalty))
    result = 2.0 * mean - exact(exact(z, better[...]), phi[...], NT)
    to_tiles(result, tiles2)
    end2 = scatter(tiles2, received2, scatter_send2, scatter_recv2)
    after[...] = result

    @pl.when(me < owners)
    def _():
        arrivals(tiles2, received2, scatter_send2, scatter_recv2)
        mine = tiles2[pl.ds(me * chunk, chunk)]
        others = received2[1:slabs]
        old = gathered[me]
        new = (mine + others.sum(0)) * (1.0 / slabs)
        primal = total(jnp.square(mine - new)) + total(jnp.square(others - new[None]))
        dual = (slabs * penalty * penalty) * total(jnp.square(new - old))
        sub = lax.broadcasted_iota(jnp.int32, (8, 128), 0)
        lane = lax.broadcasted_iota(jnp.int32, (8, 128), 1)
        top = jnp.where(lane == 0, stats[0], jnp.broadcast_to(primal, (8, 128)))
        low = jnp.where(lane == 0, stats[1], jnp.broadcast_to(dual, (8, 128)))
        gathered2[me, 0:chunk] = new
        gathered2[me, chunk] = jnp.where(sub == 0, top, low)
        spread(gathered2, gather_send2, gather_recv2)
        for f in range(1, feats):

            def outward(d, f=f):
                copy(
                    gathered2.at[me, chunk], foreign.at[f - 1, me], foreign_send.at[f - 1, d],
                    foreign_recv.at[f - 1, me], peer(d), feat_of(f),
                ).start()

            each(0, slabs, outward)

    collected(gathered2, gather_send2, gather_recv2)
    new = from_tiles(lambda t: gathered2[t // chunk, t % chunk], rows, columns)
    last[...] = new
    change = (first - mean) + (result - new)
    duals[...] = change
    sums = gathered2[0, chunk]
    for o in range(1, owners):
        sums = sums + gathered2[o, chunk]
    for f in range(1, feats):

        def inward(o, f=f):
            copy(
                gathered2.at[0, chunk], foreign.at[f - 1, o], foreign_send.at[f - 1, 0],
                foreign_recv.at[f - 1, o], me, core,
            ).wait_recv()

        each(0, owners, inward)
        for o in range(owners):
            sums = sums + foreign[f - 1, o]
    history[...] = jnp.sqrt(sums * (1.0 / (slabs * reduced * width)))

    each(1, slabs, end1)
    each(1, slabs, end2)

    @pl.when(me < owners)
    def _():
        def leave(d):
            copy(gathered.at[me], gathered.at[me], gather_send.at[d], gather_recv.at[me], peer(d), core).wait_send()
            copy(
                gathered2.at[me], gathered2.at[me], gather_send2.at[d], gather_recv2.at[me], peer(d), core
            ).wait_send()

        each(1, slabs, leave)
        for f in range(1, feats):

            def depart(d, f=f):
                copy(
                    gathered2.at[me, chunk], foreign.at[f - 1, me], foreign_send.at[f - 1, d],
                    foreign_recv.at[f - 1, me], peer(d), feat_of(f),
                ).wait_send()

            each(0, slabs, depart)


def last_kernel(after, duals, last, history, out_after, out_duals, out_last, out_history):
    half, width = out_last.shape
    for r in range(half):
        out_after[r] = after[r : r + 1, :width]
        out_duals[r] = duals[r : r + 1, :width]
    out_last[...] = last[:half, :width]
    out_history[...] = history[0:2, 0:2]


LIMIT = 20 * 2**20


def up(value, step):
    return -(-value // step) * step


def shards(states, inputs, targets):
    reduced = states.shape[0]
    feats = lax.axis_size("feat")
    slabs = lax.axis_size("slab")
    half = reduced // feats
    width = reduced + reduced * (reduced + 1) // 2 + 2
    count = states.shape[1] * feats
    rows, columns = up(half, 8), up(width, 128)
    pieces = (rows // 8) * (columns // 128)
    chunk = -(-pieces // slabs)
    owners = -(-pieces // chunk)
    f32 = jnp.float32
    packed = lax.all_gather(jnp.concatenate([states, targets, inputs[None]], 0), "feat", axis=1, tiled=True)
    vmem = pl.BlockSpec(memory_space=pltpu.VMEM)
    square = jax.ShapeDtypeStruct((count, count), f32)
    system, inverse = pl.pallas_call(
        functools.partial(first_kernel, reduced=reduced),
        out_shape=(square, square),
        in_specs=[vmem],
        out_specs=(vmem,) * 2,
        scratch_shapes=[pltpu.VMEM((count, count), f32)],
        compiler_params=pltpu.CompilerParams(vmem_limit_bytes=LIMIT),
        name="local_inverse",
    )(packed)
    shard = jax.ShapeDtypeStruct((half, width), f32)
    spread_rows = jax.ShapeDtypeStruct((half, 1, width), f32)
    block = jax.ShapeDtypeStruct((rows, columns), f32)
    dma = pltpu.SemaphoreType.DMA
    after, duals, last, history = pl.pallas_call(
        functools.partial(second_kernel, reduced=reduced, width=width),
        out_shape=(block, block, block, jax.ShapeDtypeStruct((8, 128), f32)),
        in_specs=[vmem] * 3,
        out_specs=(vmem,) * 4,
        scratch_shapes=[
            pltpu.VMEM((rows, columns), f32),
            pltpu.VMEM((owners * chunk, 8, 128), f32),
            pltpu.VMEM((columns, count), f32),
            pltpu.VMEM((rows, count), f32),
            pltpu.VMEM((count, count), f32),
            pltpu.VMEM((slabs, chunk, 8, 128), f32),
            pltpu.VMEM((owners, chunk, 8, 128), f32),
            pltpu.VMEM((slabs, chunk, 8, 128), f32),
            pltpu.VMEM((owners, chunk + 1, 8, 128), f32),
            pltpu.VMEM((max(feats - 1, 1), owners, 8, 128), f32),
            pltpu.VMEM((owners * chunk, 8, 128), f32),
            pltpu.VMEM((2, 8, 128), f32),
            dma((slabs,)), dma((slabs,)), dma((slabs,)), dma((owners,)),
            dma((slabs,)), dma((slabs,)), dma((slabs,)), dma((owners,)),
            dma((max(feats - 1, 1), slabs)), dma((max(feats - 1, 1), owners)),
        ],
        compiler_params=pltpu.CompilerParams(vmem_limit_bytes=LIMIT, collective_id=0, has_side_effects=True),
        name="second_and_averages",
    )(packed, system, inverse)
    after, duals, last, history = pl.pallas_call(
        last_kernel,
        out_shape=(spread_rows, spread_rows, shard, jax.ShapeDtypeStruct((2, 2), f32)),
        in_specs=[vmem] * 4,
        out_specs=(vmem,) * 4,
        compiler_params=pltpu.CompilerParams(vmem_limit_bytes=4 * 2**20),
        name="outputs",
    )(after, duals, last, history)
    return (jnp.swapaxes(after, 0, 1), jnp.swapaxes(duals, 0, 1), last, history)


def solution(mesh):
    in_specs = (P(None, ("slab", "feat")), P(("slab", "feat")), P(None, ("slab", "feat")))
    out_specs = (P("slab", "feat", None), P("slab", "feat", None), P("feat", None), P())
    return jax.shard_map(shards, mesh=mesh, in_specs=in_specs, out_specs=out_specs, check_vma=False)
```

profile of v0, /device:TPU:0, one launch (start us, length us, event | category | flops | bytes accessed | tf_op | source)
XLA Modules:
  0.0 43.8 jit_solution(5464024708370674483)
XLA Ops:
  0.6 0.0 copy-start
  0.6 0.7 %copy-done = f32[256]{0:T(256)S(1)} copy-done((f32[256]{0:T(256)S(1)}, f32[256]{0:T(256)}, u32[]{:S(2)}) %copy-start) | copy-done | bytes 1048
  1.3 0.8 %pad_maximum_fusion = f32[81,256]{1,0:T(8,128)S(1)} fusion(f32[1,256]{1,0:T(1,128)S(1)} %bitcast.3, f32[40,256]{1,0:T(8,128)} %param.5, f32[40,256]{1,0:T(8,128)} %param.3), kind=kLoop, calls=%fused_computation | loop fusion | flops 41472 | bytes 165888 | tf_op jit(solution)/shard_map/concatenate | solution.py:382
  2.1 2.1 %all_gather.3.packed = f32[81,512]{1,0:T(8,128)S(1)} all-gather(f32[81,256]{1,0:T(8,128)S(1)} %pad_maximum_fusion), channel_id=1, replica_groups=mesh['slab'=16,'feat'=2] {'feat'}, dimensions={1}, use_global_device_ids=true | all-gather | bytes 248832 | tf_op jit(solution)/shard_map/all_gather | solution.py:382
  4.2 8.2 %local_inverse.1 = (f32[512,512]{1,0:T(8,128)S(1)}, f32[512,512]{1,0:T(8,128)S(1)}) custom-call(f32[81,512]{1,0:T(8,128)S(1)} %all_gather.3.packed), custom_call_target="tpu_custom_call" | custom-call | tf_op jit(solution)/shard_map/local_inverse/pallas_call | solution.py:385
  12.4 30.7 %second_and_averages.1 = (f32[24,896]{1,0:T(8,128)S(1)}, f32[24,896]{1,0:T(8,128)S(1)}, f32[24,896]{1,0:T(8,128)S(1)}, f32[8,128]{1,0:T(8,128)S(1)}) custom-call(f32[81,512]{1,0:T(8,128)S(1)} %all_gather.3.packed, f32[512,512]{1,0:T(8,128)S(1)} %get-tuple-element.14.system, f32[512,512]{1,0:T(8,128)S(1)} %get-tuple-element.15.inverse), custom_call_target="tpu_custom_call" | custom-call | tf_op jit(solution)/shard_map/second_and_averages/pallas_call | solution.py:398
  43.1 0.7 %outputs.1 = (f32[20,1,862]{2,1,0:T(1,128)}, f32[20,1,862]{2,1,0:T(1,128)}, f32[20,862]{1,0:T(8,128)}, f32[2,2]{1,0:T(2,128)}) custom-call(f32[24,896]{1,0:T(8,128)S(1)} %get-tuple-element.16.after, f32[24,896]{1,0:T(8,128)S(1)} %get-tuple-element.17.duals, f32[24,896]{1,0:T(8,128)S(1)} %get-tuple-element.18.last, f32[8,128]{1,0:T(8,128)S(1)} %get-tuple-element.19.history), custom_call_target="tpu_custom_call" | custom-call | tf_op jit(solution)/shard_map/outputs/pallas_call | solution.py:423
Async XLA Ops:
  0.6 0.7 %copy-start = (f32[256]{0:T(256)S(1)}, f32[256]{0:T(256)}, u32[]{:S(2)}) copy-start(f32[256]{0:T(256)} %param.4) | copy-start | bytes 3076
where the time goes:
time: 44.2 us; the launch traced here: 43.8 us
  Pallas kernels  39.6 us (90%)
  blocking collectives  2.06 us (5%)
  other arithmetic  0.81 us (2%)
  local copies, waits for them, and re-layouts  0.67 us (2%)
  between operations  0.66 us (1%)
    pallas_call x1, Pallas kernels, shards(): pl.pallas_call(functools.partial(second_kernel, reduced=reduced, width=wi...  30.7 us
    pallas_call x1, Pallas kernels, shards(): pl.pallas_call(functools.partial(first_kernel, reduced=reduced), out_shap...  8.17 us
    all_gather x1, blocking collectives, shards(): lax.all_gather(jnp.concatenate([states, targets, inputs[None]], 0), 'feat...  2.06 us

commit v1 on v0

v1 whole, which is shorter than its diff:
```python
import functools

import jax
import jax.numpy as jnp
from jax import lax
from jax.experimental import pallas as pl
from jax.experimental.pallas import tpu as pltpu
from jax.sharding import PartitionSpec as P

penalty = 1.0
LIMIT = 20 * 2**20
LANES = 128
NN = (((1,), (0,)), ((), ()))
NT = (((1,), (1,)), ((), ()))
TN = (((0,), (0,)), ((), ()))
F32 = jnp.float32
BF16 = jnp.bfloat16


def up(value, step):
    return -(-value // step) * step


def dot(left, right, dims=NN):
    return lax.dot_general(left.astype(BF16), right.astype(BF16), dims, preferred_element_type=F32)


def split(value):
    high = value.astype(BF16)
    return high, (value - high.astype(F32)).astype(BF16)


def thin(left, high, low, dims=NN):
    rows = left.shape[0]
    top = left.astype(BF16).astype(F32)
    both = jnp.concatenate([top, left - top], 0).astype(BF16)
    out = dot(both, high, dims) + dot(both, low, dims)
    return out[:rows] + out[rows:]


def eye_mask(size):
    return lax.broadcasted_iota(jnp.int32, (size, size), 0) == lax.broadcasted_iota(jnp.int32, (size, size), 1)


def eye(size):
    return jnp.where(eye_mask(size), 1.0, 0.0)


def invert_by_pivots(source, target):
    size = source.shape[0]
    target[...] = source[...]
    sub = lax.broadcasted_iota(jnp.int32, (size, 1), 0)
    lane = lax.broadcasted_iota(jnp.int32, (1, size), 1)

    def step(k, carry):
        row = target[pl.ds(k, 1), :]
        here = lane == k
        pivot = jnp.sum(jnp.where(here, row, 0.0), axis=1, keepdims=True)
        scaled = jnp.where(here, 1.0, row) / pivot
        whole = target[...]
        column = jnp.sum(jnp.where(here, whole, 0.0), axis=1, keepdims=True)
        column = jnp.where(sub == k, -1.0, column)
        kept = jnp.where(here | (sub == k), 0.0, whole)
        target[...] = kept - column * scaled
        return carry

    lax.fori_loop(0, size, step, 0)


def exchange_kernel(states, inputs, targets, packed, far_s, far_u, far_t, send, recv):
    feats = lax.axis_size("feat")
    core = lax.axis_index("feat")
    reduced, own = states.shape
    half = reduced // feats
    scale = 1.0 / (own * feats)

    def moves(f):
        peer = lax.rem(core + f, feats)
        pairs = ((states, far_s), (inputs, far_u), (targets, far_t))
        return [
            pltpu.make_async_remote_copy(
                src_ref=source, dst_ref=target.at[f - 1], send_sem=send.at[f - 1, i], recv_sem=recv.at[f - 1, i],
                device_id={"feat": peer}, device_id_type=pl.DeviceIdType.MESH,
            )
            for i, (source, target) in enumerate(pairs)
        ]

    def place(f, s, u, t):
        spot = slice(f * own, (f + 1) * own)
        packed[0:reduced, spot] = s[...]
        packed[packed.shape[0] - 1 :, spot] = u[...]
        for c in range(feats):

            @pl.when(core == c)
            def _():
                packed[reduced : reduced + half, spot] = t[c * half : (c + 1) * half, :] * scale

    barrier = pltpu.get_barrier_semaphore()
    for f in range(1, feats):
        pl.semaphore_signal(
            barrier, inc=1, device_id={"feat": lax.rem(core + f, feats)}, device_id_type=pl.DeviceIdType.MESH
        )
    pl.semaphore_wait(barrier, feats - 1)
    for f in range(1, feats):
        for move in moves(f):
            move.start()
    rest = packed.shape[0] - 1 - reduced - half
    packed[reduced + half : reduced + half + rest, :] = jnp.zeros((rest, packed.shape[1]), F32)
    place(0, states, inputs, targets)
    for f in range(1, feats):
        for move in moves(f):
            move.wait_recv()
        place(f, far_s.at[f - 1], far_u.at[f - 1], far_t.at[f - 1])
    for f in range(1, feats):
        for move in moves(f):
            move.wait_send()


def stacked_gram(value, orders):
    parts = []
    rest = value
    for _ in range(1 + max(max(order) for order in orders)):
        high = rest.astype(BF16).astype(F32)
        parts.append(high)
        rest = rest - high
    left = jnp.concatenate([parts[i] for i, _ in orders], 0)
    right = jnp.concatenate([parts[j] for _, j in orders], 0)
    return dot(left, right, TN)


def inverse_kernel(packed, high_a, low_a, inverse, high_x, low_x, y, r, system, shifted, *, reduced, half):
    count = packed.shape[1]
    rows = y.shape[0]
    s = packed[0:reduced, :]
    signal = packed[packed.shape[0] - 1 :, :]
    inner = stacked_gram(s, ((0, 0), (0, 1), (1, 0), (0, 2), (2, 0), (1, 1)))
    extra = jnp.concatenate([s * s * (0.5**0.5), jnp.broadcast_to(signal, (8, count)) * (8.0**-0.5)], 0)
    a = inner + 0.5 * inner * inner + stacked_gram(extra, ((0, 0), (0, 1), (1, 0))) + 1.0
    a = a * (1.0 / count) + jnp.where(eye_mask(count), penalty, 0.0)
    system[...] = a
    high_a[...], low_a[...] = split(a)

    high = jnp.max(jnp.sum(jnp.abs(a), axis=0, keepdims=True)) / penalty
    delta = (high - 1.0) / (high + 1.0)
    alpha = 2.0 / ((1.0 + high) * penalty)
    c = 2.0 / (2.0 - delta * delta)
    inverse[...] = (c * alpha) * (jnp.where(eye_mask(count), 2.0, 0.0) - alpha * a)
    delta = delta * delta / (2.0 - delta * delta)

    def coarse(state):
        step, delta = state
        x = inverse[...].astype(BF16)
        shifted[...] = dot(high_a[...], x).astype(BF16)
        c = 2.0 / (2.0 - delta * delta)
        inverse[...] = c * (2.0 * inverse[...] - dot(x, shifted[...]))
        return step + 1, delta * delta / (2.0 - delta * delta)

    lax.while_loop(lambda state: (state[1] > 0.1) & (state[0] < 12), coarse, (0, delta))

    sub = lax.broadcasted_iota(jnp.int32, (rows, count), 0)
    mixed = (lax.broadcasted_iota(jnp.int32, (rows, count), 1) + 1) * (sub * 40503 + 30011)
    mixed = (mixed ^ (mixed >> 7)) * 9973
    signs = jnp.where(((mixed >> 9) & 1) == 1, 1.0, -1.0)
    b = jnp.where(sub < half, packed[reduced : reduced + rows, :], signs)

    def solve():
        high_x[...], low_x[...] = split(inverse[...])
        first = thin(b, high_x[...], low_x[...])
        left = b - thin(first, high_a[...], low_a[...])
        y[...] = first
        r[...] = left
        return jnp.sum(jnp.where(sub < half, 0.0, left * left)) * (1.0 / (rows - half))

    x = inverse[...].astype(BF16)
    shifted[...] = (eye(count) - (dot(high_a[...], x) + dot(low_a[...], x))).astype(BF16)
    inverse[...] = x.astype(F32) + dot(x, shifted[...])

    def polish(state):
        step, _ = state
        xh, xl = high_x[...], low_x[...]
        gap = eye(count) - (dot(high_a[...], xh) + (dot(high_a[...], xl) + dot(low_a[...], xh)))
        shifted[...] = gap.astype(BF16)
        inverse[...] = inverse[...] + dot(xh, shifted[...])
        return step + 1, solve()

    _, worst = lax.while_loop(
        lambda state: jnp.logical_not(state[1] < 0.01) & (state[0] < 6), polish, (0, solve())
    )

    @pl.when(jnp.logical_not(worst < 0.01))
    def _():
        invert_by_pivots(system, inverse)
        solve()


def build_features(packed, phi, reduced):
    count = packed.shape[1]
    row = reduced
    phi[0:reduced, :] = packed[0:reduced, :]
    for i in range(reduced):
        phi[row : row + reduced - i, :] = packed[i : i + 1, :] * packed[i:reduced, :]
        row += reduced - i
    phi[row : row + 1, :] = packed[packed.shape[0] - 1 :, :]
    phi[row + 1 : row + 2, :] = jnp.ones((1, count), F32)
    if row + 2 < phi.shape[0]:
        phi[row + 2 :, :] = jnp.zeros((phi.shape[0] - row - 2, count), F32)


def total(value):
    flat = value.reshape(-1, value.shape[-1])
    return jnp.sum(jnp.sum(flat, axis=0, keepdims=True), axis=1, keepdims=True)


def second_kernel(
    packed, high_a, low_a, inverse, high_x, low_x, y, r, after, duals, last, history,
    phi, high_p, low_p, high_w, low_w, better, high_b, low_b, gap,
    own1, own2, land1, land2, out1, out2, mean1, mean2,
    send1, recv1, spread1, got1, send2, recv2, spread2, got2,
    *, reduced, half, width,
):
    slabs = lax.axis_size("slab")
    feats = lax.axis_size("feat")
    me = lax.axis_index("slab")
    core = lax.axis_index("feat")
    owners, _, wide = own1.shape
    base = (slabs - owners) // 2
    head = feats - 1
    rows, count = y.shape
    spot = jnp.clip(me - base, 0, owners - 1)
    owning = (core == head) & (me >= base) & (me < base + owners)

    def copy(source, target, send, recv, slab, feat):
        return pltpu.make_async_remote_copy(
            src_ref=source, dst_ref=target, send_sem=send, recv_sem=recv,
            device_id={"slab": slab, "feat": feat}, device_id_type=pl.DeviceIdType.MESH,
        )

    def each(first, stop, body):
        if stop - first <= 16:
            for d in range(first, stop):
                body(d)
            return

        def step(d, carry):
            body(d)
            return carry

        lax.fori_loop(first, stop, step, 0)

    def everyone(body):
        for f in range(feats):

            def one(d, f=f):
                body(lax.rem(me + d, slabs), lax.rem(core + f, feats), f, d)

            each(1 if f == 0 else 0, slabs, one)

    barrier = pltpu.get_barrier_semaphore()

    def greet(slab, feat):
        pl.semaphore_signal(
            barrier, inc=1, device_id={"slab": slab, "feat": feat}, device_id_type=pl.DeviceIdType.MESH
        )

    @pl.when(owning)
    def _():
        everyone(lambda slab, feat, f, d: greet(slab, feat))

    @pl.when(jnp.logical_not(owning))
    def _():
        each(0, owners, lambda k: greet(base + k, head))

    b = packed[reduced : reduced + rows, :]
    ah, al, xh, xl = high_a[...], low_a[...], high_x[...], low_x[...]
    answer = y[...] + thin(r[...], xh, xl)
    real = lax.broadcasted_iota(jnp.int32, (rows, 1), 0) < half
    build_features(packed, phi, reduced)
    high_p[...], low_p[...] = split(phi[...])
    left = jnp.where(real, b - thin(answer, ah, al), 0.0)
    answer = answer + thin(left, xh, xl)
    start_value = thin(answer, high_p[...], low_p[...], NT)
    for k in range(owners):
        own1[k] = start_value[:half, k * wide : (k + 1) * wide]

    @pl.when(owning)
    def _():
        pl.semaphore_wait(barrier, slabs * feats - 1)

    @pl.when(jnp.logical_not(owning))
    def _():
        pl.semaphore_wait(barrier, owners)

    def other(k):
        return jnp.logical_not((core == head) & (me == base + k))

    def scatter(source, landing, send, recv):
        def piece(k):
            return copy(source.at[k], landing.at[core, me], send.at[k], recv.at[core, me], base + k, head)

        def start(k):
            @pl.when(other(k))
            def _():
                piece(k).start()

        def finish(k):
            @pl.when(other(k))
            def _():
                piece(k).wait_send()

        each(0, owners, start)
        return finish

    def arrivals(source, landing, send, recv):
        landing[head, me] = source[spot]

        def wait(slab, feat, f, d):
            copy(source.at[0], landing.at[feat, slab], send.at[0], recv.at[feat, slab], me, core).wait_recv()

        everyone(wait)

    def spread(source, target, send, recv, wait=False):
        def one(slab, feat, f, d):
            move = copy(source.at[feat], target.at[spot], send.at[feat, slab], recv.at[spot], slab, feat)
            if wait:
                move.wait_send()
            else:
                move.start()

        everyone(one)

    def collected(source, target, send, recv):
        def wait(k):
            @pl.when(other(k))
            def _():
                copy(source.at[0], target.at[k], send.at[0, 0], recv.at[k], me, core).wait_recv()

        each(0, owners, wait)

    end1 = scatter(own1, land1, send1, recv1)

    gap[...] = (eye(count) - (dot(ah, xh) + (dot(ah, xl) + dot(al, xh)))).astype(BF16)
    better[...] = inverse[...] + dot(xh, gap[...])
    high_b[...], low_b[...] = split(better[...])
    bh, bl = high_b[...], low_b[...]
    gap[...] = (eye(count) - (dot(ah, bh) + (dot(ah, bl) + dot(al, bh)))).astype(BF16)
    better[...] = better[...] + dot(bh, gap[...])
    high_b[...], low_b[...] = split(better[...])

    @pl.when(owning)
    def _():
        arrivals(own1, land1, send1, recv1)
        for f in range(feats):
            out1[f] = land1[f].sum(0) * (1.0 / slabs)
        spread(out1, mean1, spread1, got1)
        mean1[spot] = out1[head]

    weights = dot(high_b[...], high_p[...], NT) + (
        dot(high_b[...], low_p[...], NT) + dot(low_b[...], high_p[...], NT)
    )
    high_w[...], low_w[...] = split(weights)
    collected(out1, mean1, spread1, got1)

    def joined(buffer):
        whole = jnp.concatenate([buffer[k][:half] for k in range(owners)], 1)
        return jnp.concatenate([whole, jnp.zeros((rows - half, whole.shape[1]), F32)], 0)

    first = joined(own1)
    mean = joined(mean1)
    v = thin(mean, high_p[...], low_p[...]) * (2.0 / (count * penalty)) + answer
    result = first + 2.0 * mean - thin(v, high_w[...], low_w[...])
    for k in range(owners):
        own2[k] = result[:half, k * wide : (k + 1) * wide]
    end2 = scatter(own2, land2, send2, recv2)
    after[...] = result

    @pl.when(owning)
    def _():
        primal1 = jnp.zeros((1, 1), F32)
        dual1 = jnp.zeros((1, 1), F32)
        for f in range(feats):
            primal1 = primal1 + total(jnp.square(land1[f] - out1[f][None]))
            dual1 = dual1 + total(jnp.square(out1[f]))
        arrivals(own2, land2, send2, recv2)
        primal2 = jnp.zeros((1, 1), F32)
        dual2 = jnp.zeros((1, 1), F32)
        for f in range(feats):
            new = land2[f].sum(0) * (1.0 / slabs)
            out2[f, 0:half] = new
            primal2 = primal2 + total(jnp.square(land2[f] - new[None]))
            dual2 = dual2 + total(jnp.square(new - out1[f]))
        scale = slabs * penalty * penalty
        lane = lax.broadcasted_iota(jnp.int32, (1, wide), 1)
        sums = jnp.where(lane == 0, primal1, jnp.where(lane == 1, primal2, 0.0))
        sums = jnp.where(lane == 2, dual1 * scale, jnp.where(lane == 3, dual2 * scale, sums))
        for f in range(feats):
            out2[f, half : half + 1] = sums
        spread(out2, mean2, spread2, got2)
        mean2[spot] = out2[head]

    each(0, owners, end1)
    each(0, owners, end2)

    @pl.when(owning)
    def _():
        spread(out1, mean1, spread1, got1, wait=True)

    collected(out2, mean2, spread2, got2)
    new = joined(mean2)
    last[...] = new
    duals[...] = (first - mean) + (result - new)
    sums = mean2[0][half : half + 1]
    for k in range(1, owners):
        sums = sums + mean2[k][half : half + 1]
    roots = jnp.sqrt(sums[:, 0:LANES] * (1.0 / (slabs * reduced * width)))
    history[...] = jnp.broadcast_to(roots, history.shape)

    @pl.when(owning)
    def _():
        spread(out2, mean2, spread2, got2, wait=True)


def last_kernel(after, duals, last, history, out_after, out_duals, out_last, out_history):
    half, width = out_last.shape
    for r in range(half):
        out_after[r] = after[r : r + 1, :width]
        out_duals[r] = duals[r : r + 1, :width]
    out_last[...] = last[:half, :width]
    out_history[0:1, :] = history[0:1, 0:2]
    out_history[1:2, :] = history[0:1, 2:4]


def shards(states, inputs, targets):
    reduced, own = states.shape
    feats = lax.axis_size("feat")
    slabs = lax.axis_size("slab")
    half = reduced // feats
    width = reduced + reduced * (reduced + 1) // 2 + 2
    count = own * feats
    rows = up(half + 1, 8)
    tiles = up(width, LANES) // LANES
    wide = -(-tiles // slabs) * LANES
    columns = up(width, wide)
    owners = columns // wide
    vmem = pl.BlockSpec(memory_space=pltpu.VMEM)
    dma = pltpu.SemaphoreType.DMA

    def shape(*sizes, dtype=F32):
        return jax.ShapeDtypeStruct(sizes, dtype)

    def hold(*sizes, dtype=F32):
        return pltpu.VMEM(sizes, dtype)

    others = max(feats - 1, 1)
    packed = pl.pallas_call(
        exchange_kernel,
        out_shape=shape(reduced + rows + 1, count),
        in_specs=[vmem] * 3,
        out_specs=vmem,
        scratch_shapes=[
            hold(others, reduced, own), hold(others, 1, own), hold(others, reduced, own),
            dma((others, 3)), dma((others, 3)),
        ],
        compiler_params=pltpu.CompilerParams(vmem_limit_bytes=LIMIT, collective_id=1, has_side_effects=True),
        name="exchange",
    )(states, inputs[None], targets)
    square = shape(count, count)
    short = shape(count, count, dtype=BF16)
    thin_shape = shape(rows, count)
    solved = pl.pallas_call(
        functools.partial(inverse_kernel, reduced=reduced, half=half),
        out_shape=(short, short, square, short, short, thin_shape, thin_shape),
        in_specs=[vmem],
        out_specs=(vmem,) * 7,
        scratch_shapes=[hold(count, count), hold(count, count, dtype=BF16)],
        compiler_params=pltpu.CompilerParams(vmem_limit_bytes=LIMIT),
        name="local_inverse",
    )(packed)
    block = shape(rows, columns)
    after, duals, last, history = pl.pallas_call(
        functools.partial(second_kernel, reduced=reduced, half=half, width=width),
        out_shape=(block, block, block, shape(8, LANES)),
        in_specs=[vmem] * 8,
        out_specs=(vmem,) * 4,
        scratch_shapes=[
            hold(columns, count),
            hold(columns, count, dtype=BF16), hold(columns, count, dtype=BF16),
            hold(count, columns, dtype=BF16), hold(count, columns, dtype=BF16),
            hold(count, count), hold(count, count, dtype=BF16), hold(count, count, dtype=BF16),
            hold(count, count, dtype=BF16),
            hold(owners, half, wide), hold(owners, half, wide),
            hold(feats, slabs, half, wide), hold(feats, slabs, half, wide),
            hold(feats, half, wide), hold(feats, half + 1, wide),
            hold(owners, half, wide), hold(owners, half + 1, wide),
            dma((owners,)), dma((feats, slabs)), dma((feats, slabs)), dma((owners,)),
            dma((owners,)), dma((feats, slabs)), dma((feats, slabs)), dma((owners,)),
        ],
        compiler_params=pltpu.CompilerParams(vmem_limit_bytes=2 * LIMIT, collective_id=0, has_side_effects=True),
        name="second_and_averages",
    )(packed, *solved)
    shard = shape(half, width)
    spread_rows = shape(half, 1, width)
    after, duals, last, history = pl.pallas_call(
        last_kernel,
        out_shape=(spread_rows, spread_rows, shard, shape(2, 2)),
        in_specs=[vmem] * 4,
        out_specs=(vmem,) * 4,
        compiler_params=pltpu.CompilerParams(vmem_limit_bytes=4 * 2**20),
        name="outputs",
    )(after, duals, last, history)
    return (jnp.swapaxes(after, 0, 1), jnp.swapaxes(duals, 0, 1), last, history)


def solution(mesh):
    in_specs = (P(None, ("slab", "feat")), P(("slab", "feat")), P(None, ("slab", "feat")))
    out_specs = (P("slab", "feat", None), P("slab", "feat", None), P("feat", None), P())
    return jax.shard_map(shards, mesh=mesh, in_specs=in_specs, out_specs=out_specs, check_vma=False)
```

time: 44.2 us -> 37.6 us (0.85); the launches traced: 43.8 us -> 38.2 us
  Pallas kernels: 39.6 us -> 35.3 us
  blocking collectives: 2.06 us -> 0 us
  local copies, waits for them, and re-layouts: 0.67 us -> 2.23 us
  other arithmetic: 0.81 us -> 0 us
    pallas_call x3 -> x4, Pallas kernels: 39.6 us -> 35.3 us  [the longest x1 27.1 us: shards(): pl.pallas_call(functools.partial(second_kernel, reduced=reduced, half=hal...]
    all_gather x1 -> x0, blocking collectives: 2.06 us -> none  [shards(): lax.all_gather(jnp.concatenate([states, targets, inputs[None]], 0), 'feat...]
    unnamed x2 -> x6, local copies, waits for them, and re-layouts: 0.67 us -> 2.23 us
    concatenate x1 -> x0, other arithmetic: 0.81 us -> none  [shards(): jnp.concatenate([states, targets, inputs[None]], 0)]
where the time goes in v1:
time: 37.6 us; the launch traced here: 38.2 us
  Pallas kernels  35.3 us (94%)
  local copies, waits for them, and re-layouts  2.23 us (6%)
  between operations  0.67 us (2%)
    pallas_call x1, Pallas kernels, shards(): pl.pallas_call(functools.partial(second_kernel, reduced=reduced, half=hal...  27.1 us
    pallas_call x1, Pallas kernels, shards(): pl.pallas_call(functools.partial(inverse_kernel, reduced=reduced, half=ha...  5.99 us
    unnamed x6, local copies, waits for them, and re-layouts  2.23 us
    pallas_call x1, Pallas kernels, shards(): pl.pallas_call(exchange_kernel, out_shape=shape(reduced + rows + 1, count...  1.47 us

profile of v1, /device:TPU:0, one launch (start us, length us, event | category | flops | bytes accessed | tf_op | source)
XLA Modules:
  0.0 38.2 jit_solution(11895534428454540627)
XLA Ops:
  0.6 0.0 copy-start.2
  0.6 0.7 %copy-done.2 = f32[256]{0:T(256)S(1)} copy-done((f32[256]{0:T(256)S(1)}, f32[256]{0:T(256)}, u32[]{:S(2)}) %copy-start.2) | copy-done | bytes 1048
  1.3 0.0 copy-start
  1.3 0.8 %copy-done = f32[40,256]{1,0:T(8,128)S(1)} copy-done((f32[40,256]{1,0:T(8,128)S(1)}, f32[40,256]{1,0:T(8,128)}, u32[]{:S(2)}) %copy-start) | copy-done | bytes 40984
  2.1 0.0 copy-start.1
  2.1 0.8 %copy-done.1 = f32[40,256]{1,0:T(8,128)S(1)} copy-done((f32[40,256]{1,0:T(8,128)S(1)}, f32[40,256]{1,0:T(8,128)}, u32[]{:S(2)}) %copy-start.1) | copy-done | bytes 40984
  2.9 1.5 %exchange.1.packed = f32[65,512]{1,0:T(8,128)S(1)} custom-call(f32[40,256]{1,0:T(8,128)S(1)} %copy-done, f32[1,256]{1,0:T(1,128)S(1)} %bitcast.3, f32[40,256]{1,0:T(8,128)S(1)} %copy-done.1), custom_call_target="tpu_custom_call" | custom-call | tf_op jit(solution)/shard_map/exchange/pallas_call | solution.py:454
  4.3 6.0 %local_inverse.1 = (bf16[512,512]{1,0:T(8,128)(2,1)S(1)}, bf16[512,512]{1,0:T(8,128)(2,1)S(1)}, f32[512,512]{1,0:T(8,128)S(1)}, bf16[512,512]{1,0:T(8,128)(2,1)S...) custom-call(f32[65,512]{1,0:T(8,128)S(1)} %exchange.1.packed), custom_call_target="tpu_custom_call" | custom-call | tf_op jit(solution)/shard_map/local_inverse/pallas_call | solution.py:469
  10.3 27.1 %second_and_averages.1 = (f32[24,896]{1,0:T(8,128)S(1)}, f32[24,896]{1,0:T(8,128)S(1)}, f32[24,896]{1,0:T(8,128)S(1)}, f32[8,128]{1,0:T(8,128)S(1)}) custom-call(f32[65,512]{1,0:T(8,128)S(1)} %exchange.1.packed, bf16[512,512]{1,0:T(8,128)(2,1)S(1)} %get-tuple-element.19.high_a, bf16[512,512]{1,0:T(8,128)(2,1)S(1)} %get-tuple-element.20.low_a, ...), custom_call_target="tpu_custom_call" | custom-call | tf_op jit(solution)/shard_map/second_and_averages/pallas_call | solution.py:479
  37.5 0.7 %outputs.1 = (f32[20,1,862]{2,1,0:T(1,128)}, f32[20,1,862]{2,1,0:T(1,128)}, f32[20,862]{1,0:T(8,128)}, f32[2,2]{1,0:T(2,128)}) custom-call(f32[24,896]{1,0:T(8,128)S(1)} %get-tuple-element.26.after, f32[24,896]{1,0:T(8,128)S(1)} %get-tuple-element.27.duals, f32[24,896]{1,0:T(8,128)S(1)} %get-tuple-element.28.last, f32[8,128]{1,0:T(8,128)S(1)} %get-tuple-element.29.history), custom_call_target="tpu_custom_call" | custom-call | tf_op jit(solution)/shard_map/outputs/pallas_call | solution.py:502
Async XLA Ops:
  0.6 0.7 %copy-start.2 = (f32[256]{0:T(256)S(1)}, f32[256]{0:T(256)}, u32[]{:S(2)}) copy-start(f32[256]{0:T(256)} %param.4) | copy-start | bytes 3076
  1.3 0.8 %copy-start = (f32[40,256]{1,0:T(8,128)S(1)}, f32[40,256]{1,0:T(8,128)}, u32[]{:S(2)}) copy-start(f32[40,256]{1,0:T(8,128)} %states.1) | copy-start | bytes 122884
  2.1 0.8 %copy-start.1 = (f32[40,256]{1,0:T(8,128)S(1)}, f32[40,256]{1,0:T(8,128)}, u32[]{:S(2)}) copy-start(f32[40,256]{1,0:T(8,128)} %targets.1) | copy-start | bytes 122884

commit v2 on v1

v2 whole, which is shorter than its diff:
```python
import functools

import jax
import jax.numpy as jnp
from jax import lax
from jax.experimental import pallas as pl
from jax.experimental.pallas import tpu as pltpu
from jax.sharding import PartitionSpec as P

penalty = 1.0
LIMIT = 20 * 2**20
LANES = 128
NN = (((1,), (0,)), ((), ()))
NT = (((1,), (1,)), ((), ()))
TN = (((0,), (0,)), ((), ()))
F32 = jnp.float32
BF16 = jnp.bfloat16


def up(value, step):
    return -(-value // step) * step


def dot(left, right, dims=NN):
    return lax.dot_general(left.astype(BF16), right.astype(BF16), dims, preferred_element_type=F32)


def split(value):
    high = value.astype(BF16)
    return high, (value - high.astype(F32)).astype(BF16)


def thin(left, high, low, dims=NN):
    rows = left.shape[0]
    top = left.astype(BF16).astype(F32)
    both = jnp.concatenate([top, left - top], 0).astype(BF16)
    out = dot(both, high, dims) + dot(both, low, dims)
    return out[:rows] + out[rows:]


def eye_mask(size):
    return lax.broadcasted_iota(jnp.int32, (size, size), 0) == lax.broadcasted_iota(jnp.int32, (size, size), 1)


def eye(size):
    return jnp.where(eye_mask(size), 1.0, 0.0)


def invert_by_pivots(source, target):
    size = source.shape[0]
    target[...] = source[...]
    sub = lax.broadcasted_iota(jnp.int32, (size, 1), 0)
    lane = lax.broadcasted_iota(jnp.int32, (1, size), 1)

    def step(k, carry):
        row = target[pl.ds(k, 1), :]
        here = lane == k
        pivot = jnp.sum(jnp.where(here, row, 0.0), axis=1, keepdims=True)
        scaled = jnp.where(here, 1.0, row) / pivot
        whole = target[...]
        column = jnp.sum(jnp.where(here, whole, 0.0), axis=1, keepdims=True)
        column = jnp.where(sub == k, -1.0, column)
        kept = jnp.where(here | (sub == k), 0.0, whole)
        target[...] = kept - column * scaled
        return carry

    lax.fori_loop(0, size, step, 0)


def exchange_kernel(
    states, inputs, targets, all_s, all_u, all_t, near_s, near_u, near_t, local, send, recv
):
    feats = lax.axis_size("feat")
    core = lax.axis_index("feat")
    head = feats - 1
    own = states.shape[1]
    sources = (states, inputs, targets)
    nears = (near_s, near_u, near_t)
    alls = (all_s, all_u, all_t)

    def load(i, target):
        return pltpu.make_async_copy(sources[i], target, local.at[i])

    def move(i, f):
        return pltpu.make_async_remote_copy(
            src_ref=nears[i], dst_ref=alls[i].at[:, pl.ds(f * own, own)], send_sem=send.at[i], recv_sem=recv.at[f, i],
            device_id={"feat": head}, device_id_type=pl.DeviceIdType.MESH,
        )

    barrier = pltpu.get_barrier_semaphore()

    def greet(feat):
        pl.semaphore_signal(barrier, inc=1, device_id={"feat": feat}, device_id_type=pl.DeviceIdType.MESH)

    @pl.when(core == head)
    def _():
        for i in range(3):
            load(i, alls[i].at[:, pl.ds(head * own, own)]).start()
        for f in range(head):
            greet(f)
        pl.semaphore_wait(barrier, head)
        for i in range(3):
            load(i, alls[i].at[:, pl.ds(head * own, own)]).wait()
        for f in range(head):
            for i in range(3):
                move(i, f).wait_recv()

    for f in range(head):

        @pl.when(core == f)
        def _():
            for i in range(3):
                load(i, nears[i]).start()
            greet(head)
            pl.semaphore_wait(barrier, 1)
            for i in range(3):
                load(i, nears[i]).wait()
                move(i, f).start()
            for i in range(3):
                move(i, f).wait_send()


def stacked(value, orders):
    parts = []
    rest = value
    for _ in range(1 + max(max(order) for order in orders)):
        high = rest.astype(BF16).astype(F32)
        parts.append(high)
        rest = rest - high
    left = jnp.concatenate([parts[i] for i, _ in orders], 0)
    right = jnp.concatenate([parts[j] for _, j in orders], 0)
    return left.astype(BF16), right.astype(BF16)


def inverse_kernel(all_s, all_u, high_a, low_a, inverse, high_x, low_x, system, shifted):
    reduced, count = all_s.shape
    edge = LANES
    spans = [slice(k, k + edge) for k in range(0, count, edge)]

    def solve():
        s = all_s[...]
        sub = lax.broadcasted_iota(jnp.int32, (8, count), 0)
        last = jnp.where(sub == 0, all_u[...], jnp.where(sub == 1, 1.0, 0.0)) * (1.0 / count) ** 0.5
        left, right = stacked(s * (0.5 / count) ** 0.25, ((0, 0), (0, 1), (1, 0), (0, 2), (2, 0), (1, 1)))
        extra = jnp.concatenate([s * s * (0.5 / count) ** 0.5, last], 0)
        left2, right2 = stacked(extra, ((0, 0), (0, 1), (1, 0)))
        sums = [jnp.zeros((8, edge), F32)] * len(spans)
        for p, down in enumerate(spans):
            inner = dot(left[:, down], right, TN)
            other = dot(left2[:, down], right2, TN)
            for q, across in enumerate(spans):
                part = inner[:, across]
                part = part * (part + (2.0 / count) ** 0.5) + other[:, across]
                if p == q:
                    part = part + jnp.where(eye_mask(edge), penalty, 0.0)
                system[down, across] = part
                high_a[down, across], low_a[down, across] = split(part)
                sums[q] = sums[q] + jnp.abs(part).reshape(edge // 8, 8, edge).sum(0)
        sums = functools.reduce(jnp.maximum, [jnp.sum(part, axis=0, keepdims=True) for part in sums])
        high = jnp.max(sums) / penalty
        delta = (high - 1.0) / (high + 1.0)
        alpha = 2.0 / ((1.0 + high) * penalty)
        c = 2.0 / (2.0 - delta * delta)
        for p, down in enumerate(spans):
            for q, across in enumerate(spans):
                part = (-c * alpha * alpha) * system[down, across]
                if p == q:
                    part = part + jnp.where(eye_mask(edge), 2.0 * c * alpha, 0.0)
                inverse[down, across] = part
        delta = delta * delta / (2.0 - delta * delta)

        def coarse(state):
            step, delta = state
            x = inverse[...].astype(BF16)
            shifted[...] = dot(high_a[...], x).astype(BF16)
            c = 2.0 / (2.0 - delta * delta)
            inverse[...] = c * (2.0 * inverse[...] - dot(x, shifted[...]))
            return step + 1, delta * delta / (2.0 - delta * delta)

        lax.while_loop(lambda state: (state[1] > 0.085) & (state[0] < 12), coarse, (0, delta))

        mixed = (lax.broadcasted_iota(jnp.int32, (8, count), 1) + 1) * (sub * 40503 + 30011)
        mixed = (mixed ^ (mixed >> 7)) * 9973
        signs = jnp.where(((mixed >> 9) & 1) == 1, 1.0, -1.0)

        x = inverse[...].astype(BF16)
        ah, al = high_a[...], low_a[...]
        shifted[...] = (eye(count) - (dot(ah, x) + dot(al, x))).astype(BF16)
        once = signs - thin(dot(signs, x), ah, al)
        high_once, low_once = split(once)
        twice = once - thin(dot(high_once, x) + dot(low_once, x), ah, al)
        inverse[...] = x.astype(F32) + dot(x, shifted[...])
        high_x[...], low_x[...] = split(inverse[...])
        worst = jnp.sum(twice * twice) * (1.0 / 8.0)

        def polish(state):
            step, _ = state
            ah, al, xh, xl = high_a[...], low_a[...], high_x[...], low_x[...]
            shifted[...] = (eye(count) - (dot(ah, xh) + (dot(ah, xl) + dot(al, xh)))).astype(BF16)
            once = signs - thin(thin(signs, xh, xl), ah, al)
            twice = once - thin(thin(once, xh, xl), ah, al)
            inverse[...] = inverse[...] + dot(xh, shifted[...])
            high_x[...], low_x[...] = split(inverse[...])
            return step + 1, jnp.sum(twice * twice) * (1.0 / 8.0)

        _, worst = lax.while_loop(
            lambda state: jnp.logical_not(state[1] < 0.012) & (state[0] < 6), polish, (0, worst)
        )

        @pl.when(jnp.logical_not(worst < 0.012))
        def _():
            invert_by_pivots(system, inverse)
            high_x[...], low_x[...] = split(inverse[...])

    pl.when(lax.axis_index("feat") == lax.axis_size("feat") - 1)(solve)


def build_features(all_s, all_u, phi):
    reduced, count = all_s.shape
    row = reduced
    phi[0:reduced, :] = all_s[...]
    for i in range(reduced):
        phi[row : row + reduced - i, :] = all_s[i : i + 1, :] * all_s[i:reduced, :]
        row += reduced - i
    phi[row : row + 1, :] = all_u[...]
    phi[row + 1 : row + 2, :] = jnp.ones((1, count), F32)
    if row + 2 < phi.shape[0]:
        phi[row + 2 :, :] = jnp.zeros((phi.shape[0] - row - 2, count), F32)


def lanes_of(value):
    return jnp.sum(value.reshape(-1, value.shape[-1]), axis=0, keepdims=True)


def second_kernel(
    all_s, all_u, all_t, high_a, low_a, inverse, high_x, low_x, after, duals, last, history,
    phi, high_p, low_p, high_w, low_w, better, high_b, low_b, gap, answer,
    own1, own2, land1, land2, out1, out2, mean1, mean2, mine, ship, span,
    send1, recv1, spread1, got1, send2, recv2, spread2, got2, ship_send, ship_recv,
    *, width,
):
    slabs = lax.axis_size("slab")
    feats = lax.axis_size("feat")
    me = lax.axis_index("slab")
    core = lax.axis_index("feat")
    owners, reduced, wide = own1.shape
    half = reduced // feats
    count = all_s.shape[1]
    base = (slabs - owners) // 2
    head = feats - 1
    spot = jnp.clip(me - base, 0, owners - 1)
    leading = core == head
    inside = (me >= base) & (me < base + owners)

    def copy(source, target, send, recv, slab, feat):
        return pltpu.make_async_remote_copy(
            src_ref=source, dst_ref=target, send_sem=send, recv_sem=recv,
            device_id={"slab": slab, "feat": feat}, device_id_type=pl.DeviceIdType.MESH,
        )

    def arrived(target, size, sem):
        part = target.at[pl.ds(0, size)]
        copy(part, part, sem, sem, me, core).wait_recv()

    def departed(source, size, sem):
        part = source.at[pl.ds(0, size)]
        copy(part, part, sem, sem, me, core).wait_send()

    def each(order, body):
        if len(order) <= 16:
            for d in order:
                body(d)
            return

        def step(d, carry):
            body(d)
            return carry

        lax.fori_loop(min(order), max(order) + 1, step, 0)

    far = sorted(range(1, slabs), key=lambda d: -min(d, slabs - d))

    def slab_of(d):
        return lax.rem(me + d, slabs)

    def split_on(flag, yes, no):
        pl.when(flag)(yes)
        pl.when(jnp.logical_not(flag))(no)

    barrier = pltpu.get_barrier_semaphore()

    def greet(slab, feat):
        pl.semaphore_signal(
            barrier, inc=1, device_id={"slab": slab, "feat": feat}, device_id_type=pl.DeviceIdType.MESH
        )

    @pl.when(leading & inside)
    def _():
        for f in range(feats):
            each(far, lambda d, f=f: greet(slab_of(d), f))
        for f in range(head):
            greet(me, f)

    @pl.when(jnp.logical_not(leading & inside))
    def _():
        def one(k):
            greet(base + k, head)

        each(range(owners), one)

    @pl.when(leading & jnp.logical_not(inside))
    def _():
        for f in range(head):
            greet(me, f)

    @pl.when(jnp.logical_not(leading) & jnp.logical_not(inside))
    def _():
        greet(me, head)

    def scatter(source, landing, send, recv):
        def start(k):
            @pl.when(me != base + k)
            def _():
                copy(source.at[k], landing.at[me], send, recv, base + k, head).start()

        each(range(owners), start)

    def joined(buffer, rows):
        return jnp.concatenate([buffer[k][:rows] for k in range(owners)], 1)

    def owner_first():
        land1[me] = own1[spot]
        arrived(land1, slabs - 1, recv1)
        out1[...] = land1[...].sum(0) * (1.0 / slabs)
        each(far, lambda d: copy(out1, mean1.at[spot], spread1, got1, slab_of(d), head).start())
        mean1[spot] = out1[...]

    def owner_second():
        old = out1[...]
        primal1 = lanes_of(jnp.square(land1[...] - old[None]))
        dual1 = lanes_of(jnp.square(old))
        land2[me] = own2[spot]
        arrived(land2, slabs - 1, recv2)
        new = land2[...].sum(0) * (1.0 / slabs)
        primal2 = lanes_of(jnp.square(land2[...] - new[None]))
        dual2 = lanes_of(jnp.square(new - old))
        scale = slabs * penalty * penalty
        stats = jnp.concatenate([primal1, primal2, dual1 * scale, dual2 * scale], 0)
        for f in range(feats):
            out2[f, 0:half] = new[f * half : (f + 1) * half]
            out2[f, half : half + 4] = stats
        for d in far:
            for f in range(feats):
                copy(out2.at[f], mean2.at[spot], spread2, got2, slab_of(d), f).start()
        for f in range(head):
            copy(out2.at[f], mean2.at[spot], spread2, got2, me, f).start()
        mean2[spot] = out2[head]

    def leader():
        ah, al, xh, xl = high_a[...], low_a[...], high_x[...], low_x[...]
        b = all_t[...] * (1.0 / count)
        build_features(all_s, all_u, phi)
        high_p[...], low_p[...] = split(phi[...])
        y = thin(b, xh, xl)
        y = y + thin(b - thin(y, ah, al), xh, xl)
        y = y + thin(b - thin(y, ah, al), xh, xl)
        answer[...] = y
        start_value = thin(y, high_p[...], low_p[...], NT)
        for k in range(owners):
            own1[k] = start_value[:, k * wide : (k + 1) * wide]
        split_on(
            inside,
            lambda: pl.semaphore_wait(barrier, slabs * feats - 1),
            lambda: pl.semaphore_wait(barrier, owners + feats - 1),
        )
        scatter(own1, land1, send1, recv1)

        gap[...] = (eye(count) - (dot(ah, xh) + (dot(ah, xl) + dot(al, xh)))).astype(BF16)
        better[...] = inverse[...] + dot(xh, gap[...])
        high_b[...], low_b[...] = split(better[...])
        bh, bl = high_b[...], low_b[...]
        gap[...] = (eye(count) - (dot(ah, bh) + (dot(ah, bl) + dot(al, bh)))).astype(BF16)
        better[...] = better[...] + dot(bh, gap[...])
        high_b[...], low_b[...] = split(better[...])
        pl.when(inside)(owner_first)
        weights = dot(high_b[...], high_p[...], NT) + (
            dot(high_b[...], low_p[...], NT) + dot(low_b[...], high_p[...], NT)
        )
        high_w[...], low_w[...] = split(weights)

        split_on(
            inside,
            lambda: arrived(mean1, owners - 1, got1),
            lambda: arrived(mean1, owners, got1),
        )
        first = joined(own1, reduced)
        mean = joined(mean1, reduced)
        v = thin(mean, high_p[...], low_p[...]) * (2.0 / (count * penalty)) + answer[...]
        result = first + 2.0 * mean - thin(v, high_w[...], low_w[...])
        for k in range(owners):
            own2[k] = result[:, k * wide : (k + 1) * wide]
        scatter(own2, land2, send2, recv2)
        change = (first - mean) + result
        for f in range(head):
            ship[f, 0] = result[f * half : (f + 1) * half]
            ship[f, 1] = change[f * half : (f + 1) * half]
            copy(ship.at[f], mine, ship_send.at[f], ship_recv, me, f).start()
        mine[0] = result[head * half :]
        mine[1] = change[head * half :]
        pl.when(inside)(owner_second)

        def sent(size):
            departed(own1, size, send1)
            departed(own2, size, send2)

        split_on(inside, lambda: sent(owners - 1), lambda: sent(owners))
        for f in range(head):
            copy(ship.at[f], mine, ship_send.at[f], ship_recv, me, core).wait_send()

    def follower():
        split_on(
            inside,
            lambda: pl.semaphore_wait(barrier, owners),
            lambda: pl.semaphore_wait(barrier, owners + 1),
        )
        copy(ship.at[0], mine, ship_send.at[0], ship_recv, me, core).wait_recv()

    split_on(leading, leader, follower)
    split_on(
        leading & inside,
        lambda: arrived(mean2, owners - 1, got2),
        lambda: arrived(mean2, owners, got2),
    )
    new = joined(mean2, half)
    after[...] = mine[0]
    last[...] = new
    duals[...] = mine[1] - new
    sums = mean2[0][half : half + 4]
    for k in range(1, owners):
        sums = sums + mean2[k][half : half + 4]
    sums = jnp.sum(sums, axis=1, keepdims=True)
    history[...] = jnp.broadcast_to(jnp.sqrt(sums * (1.0 / (slabs * reduced * width))), history.shape)

    @pl.when(leading & inside)
    def _():
        departed(land1, slabs - 1, spread1)
        departed(span, slabs * feats - 1, spread2)


def last_kernel(after, duals, last, history, out_after, out_duals, out_last, out_history):
    half, width = out_last.shape
    for r in range(half):
        out_after[r] = after[r : r + 1, :width]
        out_duals[r] = duals[r : r + 1, :width]
    out_last[...] = last[:, :width]
    for r in range(2):
        out_history[r : r + 1, :] = jnp.concatenate([history[2 * r + k : 2 * r + k + 1, 0:1] for k in range(2)], 1)


def shards(states, inputs, targets):
    reduced, own = states.shape
    feats = lax.axis_size("feat")
    slabs = lax.axis_size("slab")
    half = reduced // feats
    width = reduced + reduced * (reduced + 1) // 2 + 2
    count = own * feats
    tiles = up(width, LANES) // LANES
    wide = -(-tiles // slabs) * LANES
    columns = up(width, wide)
    owners = columns // wide
    vmem = pl.BlockSpec(memory_space=pltpu.VMEM)
    dma = pltpu.SemaphoreType.DMA

    def shape(*sizes, dtype=F32):
        return jax.ShapeDtypeStruct(sizes, dtype)

    def hold(*sizes, dtype=F32):
        return pltpu.VMEM(sizes, dtype)

    gathered = pl.pallas_call(
        exchange_kernel,
        out_shape=(shape(reduced, count), shape(1, count), shape(reduced, count)),
        in_specs=[pl.BlockSpec(memory_space=pltpu.HBM)] * 3,
        out_specs=(vmem,) * 3,
        scratch_shapes=[
            hold(reduced, own), hold(1, own), hold(reduced, own), dma((3,)), dma((3,)), dma((feats, 3)),
        ],
        compiler_params=pltpu.CompilerParams(vmem_limit_bytes=LIMIT, collective_id=1, has_side_effects=True),
        name="exchange",
    )(states, inputs[None], targets)
    square = shape(count, count)
    short = shape(count, count, dtype=BF16)
    solved = pl.pallas_call(
        inverse_kernel,
        out_shape=(short, short, square, short, short),
        in_specs=[vmem] * 2,
        out_specs=(vmem,) * 5,
        scratch_shapes=[hold(count, count), hold(count, count, dtype=BF16)],
        compiler_params=pltpu.CompilerParams(vmem_limit_bytes=LIMIT),
        name="local_inverse",
    )(gathered[0], gathered[1])
    block = shape(half, columns)
    after, duals, last, history = pl.pallas_call(
        functools.partial(second_kernel, width=width),
        out_shape=(block, block, block, shape(4, LANES)),
        in_specs=[vmem] * 8,
        out_specs=(vmem,) * 4,
        scratch_shapes=[
            hold(columns, count),
            hold(columns, count, dtype=BF16), hold(columns, count, dtype=BF16),
            hold(count, columns, dtype=BF16), hold(count, columns, dtype=BF16),
            hold(count, count), hold(count, count, dtype=BF16), hold(count, count, dtype=BF16),
            hold(count, count, dtype=BF16), hold(reduced, count),
            hold(owners, reduced, wide), hold(owners, reduced, wide),
            hold(slabs, reduced, wide), hold(slabs, reduced, wide),
            hold(reduced, wide), hold(feats, half + 4, wide),
            hold(owners, reduced, wide), hold(owners, half + 4, wide),
            hold(2, half, columns), hold(max(feats - 1, 1), 2, half, columns),
            hold(slabs * feats, half + 4, wide),
            dma, dma, dma, dma, dma, dma, dma, dma, dma((max(feats - 1, 1),)), dma,
        ],
        compiler_params=pltpu.CompilerParams(vmem_limit_bytes=2 * LIMIT, collective_id=0, has_side_effects=True),
        name="second_and_averages",
    )(*gathered, *solved)
    shard = shape(half, width)
    spread_rows = shape(half, 1, width)
    after, duals, last, history = pl.pallas_call(
        last_kernel,
        out_shape=(spread_rows, spread_rows, shard, shape(2, 2)),
        in_specs=[vmem] * 4,
        out_specs=(vmem,) * 4,
        compiler_params=pltpu.CompilerParams(vmem_limit_bytes=4 * 2**20),
        name="outputs",
    )(after, duals, last, history)
    return (jnp.swapaxes(after, 0, 1), jnp.swapaxes(duals, 0, 1), last, history)


def solution(mesh):
    in_specs = (P(None, ("slab", "feat")), P(("slab", "feat")), P(None, ("slab", "feat")))
    out_specs = (P("slab", "feat", None), P("slab", "feat", None), P("feat", None), P())
    return jax.shard_map(shards, mesh=mesh, in_specs=in_specs, out_specs=out_specs, check_vma=False)
```

time: 37.6 us -> 35.9 us (0.955); the launches traced: 38.2 us -> 35.6 us
  Pallas kernels: 35.3 us -> 32.7 us
    pallas_call x3, Pallas kernels: 34.6 us -> 32 us  [the longest x1 30.4 us: shards(): pl.pallas_call(functools.partial(second_kernel, width=width), out_shape=(...]
where the time goes in v2:
time: 35.9 us; the launch traced here: 35.6 us
  Pallas kernels  32.7 us (91%)
  local copies, waits for them, and re-layouts  2.23 us (6%)
  between operations  0.67 us (2%)
    pallas_call x1, Pallas kernels, shards(): pl.pallas_call(functools.partial(second_kernel, width=width), out_shape=(...  30.4 us
    unnamed x6, local copies, waits for them, and re-layouts  2.23 us
    pallas_call x1, Pallas kernels, shards(): pl.pallas_call(exchange_kernel, out_shape=(shape(reduced, count), shape(1...  1.54 us

profile of v2, /device:TPU:0, one launch (start us, length us, event | category | flops | bytes accessed | tf_op | source)
XLA Modules:
  0.0 35.6 jit_solution(7778081997602049377)
XLA Ops:
  0.6 0.0 copy-start.2
  0.6 0.7 %copy-done.2 = f32[256]{0:T(256)S(1)} copy-done((f32[256]{0:T(256)S(1)}, f32[256]{0:T(256)}, u32[]{:S(2)}) %copy-start.2) | copy-done | bytes 1048
  1.3 0.0 copy-start
  1.3 0.8 %copy-done = f32[40,256]{1,0:T(8,128)S(1)} copy-done((f32[40,256]{1,0:T(8,128)S(1)}, f32[40,256]{1,0:T(8,128)}, u32[]{:S(2)}) %copy-start) | copy-done | bytes 40984
  2.1 0.0 copy-start.1
  2.1 0.8 %copy-done.1 = f32[40,256]{1,0:T(8,128)S(1)} copy-done((f32[40,256]{1,0:T(8,128)S(1)}, f32[40,256]{1,0:T(8,128)}, u32[]{:S(2)}) %copy-start.1) | copy-done | bytes 40984
  2.9 1.5 %exchange.1 = (f32[40,512]{1,0:T(8,128)S(1)}, f32[1,512]{1,0:T(1,128)S(1)}, f32[40,512]{1,0:T(8,128)S(1)}) custom-call(f32[40,256]{1,0:T(8,128)S(1)} %copy-done, f32[1,256]{1,0:T(1,128)S(1)} %bitcast.3, f32[40,256]{1,0:T(8,128)S(1)} %copy-done.1), custom_call_target="tpu_custom_call" | custom-call | tf_op jit(solution)/shard_map/exchange/pallas_call | solution.py:480
  4.4 30.4 %second_and_averages.1 = (f32[20,896]{1,0:T(8,128)S(1)}, f32[20,896]{1,0:T(8,128)S(1)}, f32[20,896]{1,0:T(8,128)S(1)}, f32[4,128]{1,0:T(4,128)S(1)}) custom-call(f32[40,512]{1,0:T(8,128)S(1)} %get-tuple-element.20.all_s, f32[1,512]{1,0:T(1,128)S(1)} %get-tuple-element.21.all_u, f32[40,512]{1,0:T(8,128)S(1)} %get-tuple-element.22.all_t, ...), custom_call_target="tpu_custom_call" | custom-call | tf_op jit(solution)/shard_map/second_and_averages/pallas_call | solution.py:503
  34.9 0.7 %outputs.1 = (f32[20,1,862]{2,1,0:T(1,128)}, f32[20,1,862]{2,1,0:T(1,128)}, f32[20,862]{1,0:T(8,128)}, f32[2,2]{1,0:T(2,128)}) custom-call(f32[20,896]{1,0:T(8,128)S(1)} %get-tuple-element.28.after, f32[20,896]{1,0:T(8,128)S(1)} %get-tuple-element.29.duals, f32[20,896]{1,0:T(8,128)S(1)} %get-tuple-element.30.last, f32[4,128]{1,0:T(4,128)S(1)} %get-tuple-element.31.history), custom_call_target="tpu_custom_call" | custom-call | tf_op jit(solution)/shard_map/outputs/pallas_call | solution.py:527
  (1 shorter events, 0.0 us)
Async XLA Ops:
  0.6 0.7 %copy-start.2 = (f32[256]{0:T(256)S(1)}, f32[256]{0:T(256)}, u32[]{:S(2)}) copy-start(f32[256]{0:T(256)} %param.4) | copy-start | bytes 3076
  1.3 0.8 %copy-start = (f32[40,256]{1,0:T(8,128)S(1)}, f32[40,256]{1,0:T(8,128)}, u32[]{:S(2)}) copy-start(f32[40,256]{1,0:T(8,128)} %states.1) | copy-start | bytes 122884
  2.1 0.8 %copy-start.1 = (f32[40,256]{1,0:T(8,128)S(1)}, f32[40,256]{1,0:T(8,128)}, u32[]{:S(2)}) copy-start(f32[40,256]{1,0:T(8,128)} %targets.1) | copy-start | bytes 122884

commit v3 on v2

--- a/solution.py
+++ b/solution.py
@@ -10,6 +10,8 @@
 penalty = 1.0
 LIMIT = 20 * 2**20
 LANES = 128
+STEPS = 4
+EASY = 400.0
 NN = (((1,), (0,)), ((), ()))
 NT = (((1,), (1,)), ((), ()))
 TN = (((0,), (0,)), ((), ()))
@@ -132,7 +134,11 @@
     return left.astype(BF16), right.astype(BF16)
 
 
-def inverse_kernel(all_s, all_u, high_a, low_a, inverse, high_x, low_x, system, shifted):
+def newton_scale(delta):
+    return 2.0 / (2.0 - delta * delta), delta * delta / (2.0 - delta * delta)
+
+
+def inverse_kernel(all_s, all_u, high_a, low_a, inverse, info, system, shifted, high_x, low_x):
     reduced, count = all_s.shape
     edge = LANES
     spans = [slice(k, k + edge) for k in range(0, count, edge)]
@@ -160,57 +166,54 @@
         high = jnp.max(sums) / penalty
         delta = (high - 1.0) / (high + 1.0)
         alpha = 2.0 / ((1.0 + high) * penalty)
-        c = 2.0 / (2.0 - delta * delta)
+        c, later = newton_scale(delta)
         for p, down in enumerate(spans):
             for q, across in enumerate(spans):
                 part = (-c * alpha * alpha) * system[down, across]
                 if p == q:
                     part = part + jnp.where(eye_mask(edge), 2.0 * c * alpha, 0.0)
                 inverse[down, across] = part
-        delta = delta * delta / (2.0 - delta * delta)
+        hard = jnp.logical_not(high <= EASY)
+        lane = lax.broadcasted_iota(jnp.int32, (1, LANES), 1)
+        info[...] = jnp.where(lane == 0, later, jnp.where(hard, 1.0, 0.0))
+
+        @pl.when(hard)
+        def _():
+            careful(later)
+
+    def careful(delta):
+        sub = lax.broadcasted_iota(jnp.int32, (8, count), 0)
+        mixed = (lax.broadcasted_iota(jnp.int32, (8, count), 1) + 1) * (sub * 40503 + 30011)
+        mixed = (mixed ^ (mixed >> 7)) * 9973
+        signs = jnp.where(((mixed >> 9) & 1) == 1, 1.0, -1.0)
 
         def coarse(state):
             step, delta = state
             x = inverse[...].astype(BF16)
             shifted[...] = dot(high_a[...], x).astype(BF16)
-            c = 2.0 / (2.0 - delta * delta)
+            c, later = newton_scale(delta)
             inverse[...] = c * (2.0 * inverse[...] - dot(x, shifted[...]))
-            return step + 1, delta * delta / (2.0 - delta * delta)
+            return step + 1, later
 
         lax.while_loop(lambda state: (state[1] > 0.085) & (state[0] < 12), coarse, (0, delta))
-
-        mixed = (lax.broadcasted_iota(jnp.int32, (8, count), 1) + 1) * (sub * 40503 + 30011)
-        mixed = (mixed ^ (mixed >> 7)) * 9973
-        signs = jnp.where(((mixed >> 9) & 1) == 1, 1.0, -1.0)
-
-        x = inverse[...].astype(BF16)
-        ah, al = high_a[...], low_a[...]
-        shifted[...] = (eye(count) - (dot(ah, x) + dot(al, x))).astype(BF16)
-        once = signs - thin(dot(signs, x), ah, al)
-        high_once, low_once = split(once)
-        twice = once - thin(dot(high_once, x) + dot(low_once, x), ah, al)
-        inverse[...] = x.astype(F32) + dot(x, shifted[...])
-        high_x[...], low_x[...] = split(inverse[...])
-        worst = jnp.sum(twice * twice) * (1.0 / 8.0)
 
         def polish(state):
             step, _ = state
+            high_x[...], low_x[...] = split(inverse[...])
             ah, al, xh, xl = high_a[...], low_a[...], high_x[...], low_x[...]
             shifted[...] = (eye(count) - (dot(ah, xh) + (dot(ah, xl) + dot(al, xh)))).astype(BF16)
             once = signs - thin(thin(signs, xh, xl), ah, al)
             twice = once - thin(thin(once, xh, xl), ah, al)
             inverse[...] = inverse[...] + dot(xh, shifted[...])
-            high_x[...], low_x[...] = split(inverse[...])
             return step + 1, jnp.sum(twice * twice) * (1.0 / 8.0)
 
         _, worst = lax.while_loop(
-            lambda state: jnp.logical_not(state[1] < 0.012) & (state[0] < 6), polish, (0, worst)
-        )
-
-        @pl.when(jnp.logical_not(worst < 0.012))
+            lambda state: jnp.logical_not(state[1] < 0.001) & (state[0] < 8), polish, (0, jnp.float32(1e9))
+        )
+
+        @pl.when(jnp.logical_not(worst < 0.001))
         def _():
             invert_by_pivots(system, inverse)
-            high_x[...], low_x[...] = split(inverse[...])
 
     pl.when(lax.axis_index("feat") == lax.axis_size("feat") - 1)(solve)
 
@@ -233,11 +236,11 @@
 
 
 def second_kernel(
-    all_s, all_u, all_t, high_a, low_a, inverse, high_x, low_x, after, duals, last, history,
+    all_s, all_u, all_t, high_a, low_a, inverse, info, after, duals, last, history,
     phi, high_p, low_p, high_w, low_w, better, high_b, low_b, gap, answer,
     own1, own2, land1, land2, out1, out2, mean1, mean2, mine, ship, span,
     send1, recv1, spread1, got1, send2, recv2, spread2, got2, ship_send, ship_recv,
-    *, width,
+    *, width, first_owners, second_owners, order,
 ):
     slabs = lax.axis_size("slab")
     feats = lax.axis_size("feat")
@@ -246,11 +249,18 @@
     owners, reduced, wide = own1.shape
     half = reduced // feats
     count = all_s.shape[1]
-    base = (slabs - owners) // 2
     head = feats - 1
-    spot = jnp.clip(me - base, 0, owners - 1)
     leading = core == head
-    inside = (me >= base) & (me < base + owners)
+    everyones = sorted(set(first_owners) | set(second_owners))
+
+    def among(slab_list):
+        return functools.reduce(jnp.logical_or, [me == slab for slab in slab_list])
+
+    def place_in(slab_list):
+        return functools.reduce(lambda a, b: a + b, [jnp.where(me == slab, k, 0) for k, slab in enumerate(slab_list)])
+
+    inside, inside1, inside2 = among(everyones), among(first_owners), among(second_owners)
+    spot1, spot2 = place_in(first_owners), place_in(second_owners)
 
     def copy(source, target, send, recv, slab, feat):
         return pltpu.make_async_remote_copy(
@@ -303,10 +313,8 @@
 
     @pl.when(jnp.logical_not(leading & inside))
     def _():
-        def one(k):
-            greet(base + k, head)
-
-        each(range(owners), one)
+        for slab in everyones:
+            greet(slab, head)
 
     @pl.when(leading & jnp.logical_not(inside))
     def _():
@@ -317,50 +325,72 @@
     def _():
         greet(me, head)
 
-    def scatter(source, landing, send, recv):
-        def start(k):
-            @pl.when(me != base + k)
+    def scatter(source, landing, send, recv, slab_list):
+        for k, slab in enumerate(slab_list):
+
+            @pl.when(me != slab)
             def _():
-                copy(source.at[k], landing.at[me], send, recv, base + k, head).start()
-
-        each(range(owners), start)
+                copy(source.at[k], landing.at[me], send, recv, slab, head).start()
 
     def joined(buffer, rows):
         return jnp.concatenate([buffer[k][:rows] for k in range(owners)], 1)
 
     def owner_first():
-        land1[me] = own1[spot]
+        land1[me] = own1[spot1]
         arrived(land1, slabs - 1, recv1)
         out1[...] = land1[...].sum(0) * (1.0 / slabs)
-        each(far, lambda d: copy(out1, mean1.at[spot], spread1, got1, slab_of(d), head).start())
-        mean1[spot] = out1[...]
+        each(far, lambda d: copy(out1, mean1.at[spot1], spread1, got1, slab_of(d), head).start())
+        mean1[spot1] = out1[...]
 
     def owner_second():
-        old = out1[...]
-        primal1 = lanes_of(jnp.square(land1[...] - old[None]))
+        old = mean1[spot2]
         dual1 = lanes_of(jnp.square(old))
-        land2[me] = own2[spot]
+        land2[me] = own2[spot2]
         arrived(land2, slabs - 1, recv2)
-        new = land2[...].sum(0) * (1.0 / slabs)
-        primal2 = lanes_of(jnp.square(land2[...] - new[None]))
+        whole = land2[...].sum(0)
+        new = whole[:reduced] * (1.0 / slabs)
+        primal2 = lanes_of(jnp.square(land2[:, 0:reduced] - new[None]))
         dual2 = lanes_of(jnp.square(new - old))
         scale = slabs * penalty * penalty
-        stats = jnp.concatenate([primal1, primal2, dual1 * scale, dual2 * scale], 0)
+        stats = jnp.concatenate([whole[reduced : reduced + 1], primal2, dual1 * scale, dual2 * scale], 0)
         for f in range(feats):
             out2[f, 0:half] = new[f * half : (f + 1) * half]
             out2[f, half : half + 4] = stats
-        for d in far:
+
+        def one(slab):
             for f in range(feats):
-                copy(out2.at[f], mean2.at[spot], spread2, got2, slab_of(d), f).start()
-        for f in range(head):
-            copy(out2.at[f], mean2.at[spot], spread2, got2, me, f).start()
-        mean2[spot] = out2[head]
+
+                @pl.when((me != slab) | (f != head))
+                def _():
+                    copy(out2.at[f], mean2.at[spot2], spread2, got2, slab, f).start()
+
+        for slab in order:
+            one(slab)
+        mean2[spot2] = out2[head]
 
     def leader():
-        ah, al, xh, xl = high_a[...], low_a[...], high_x[...], low_x[...]
+        ah, al = high_a[...], low_a[...]
+        delta = info[0:1, 0:1]
+        kept = info[0:1, 1:2] > 0.5
+        better[...] = inverse[...]
+
+        def coarse(step, delta):
+            x = better[...].astype(BF16)
+            gap[...] = dot(high_a[...], x).astype(BF16)
+            c, later = newton_scale(delta)
+            value = better[...]
+            better[...] = jnp.where(kept, value, c * (2.0 * value - dot(x, gap[...])))
+            return later
+
+        lax.fori_loop(0, STEPS, coarse, delta)
         b = all_t[...] * (1.0 / count)
         build_features(all_s, all_u, phi)
         high_p[...], low_p[...] = split(phi[...])
+        x = better[...].astype(BF16)
+        gap[...] = (eye(count) - (dot(ah, x) + dot(al, x))).astype(BF16)
+        better[...] = jnp.where(kept, better[...], x.astype(F32) + dot(x, gap[...]))
+        high_b[...], low_b[...] = split(better[...])
+        xh, xl = high_b[...], low_b[...]
         y = thin(b, xh, xl)
         y = y + thin(b - thin(y, ah, al), xh, xl)
         y = y + thin(b - thin(y, ah, al), xh, xl)
@@ -371,25 +401,25 @@
         split_on(
             inside,
             lambda: pl.semaphore_wait(barrier, slabs * feats - 1),
-            lambda: pl.semaphore_wait(barrier, owners + feats - 1),
-        )
-        scatter(own1, land1, send1, recv1)
+            lambda: pl.semaphore_wait(barrier, len(everyones) + feats - 1),
+        )
+        scatter(own1, land1, send1, recv1, first_owners)
 
         gap[...] = (eye(count) - (dot(ah, xh) + (dot(ah, xl) + dot(al, xh)))).astype(BF16)
-        better[...] = inverse[...] + dot(xh, gap[...])
+        better[...] = better[...] + dot(xh, gap[...])
         high_b[...], low_b[...] = split(better[...])
         bh, bl = high_b[...], low_b[...]
         gap[...] = (eye(count) - (dot(ah, bh) + (dot(ah, bl) + dot(al, bh)))).astype(BF16)
         better[...] = better[...] + dot(bh, gap[...])
         high_b[...], low_b[...] = split(better[...])
-        pl.when(inside)(owner_first)
+        pl.when(inside1)(owner_first)
         weights = dot(high_b[...], high_p[...], NT) + (
             dot(high_b[...], low_p[...], NT) + dot(low_b[...], high_p[...], NT)
         )
         high_w[...], low_w[...] = split(weights)
 
         split_on(
-            inside,
+            inside1,
             lambda: arrived(mean1, owners - 1, got1),
             lambda: arrived(mean1, owners, got1),
         )
@@ -397,9 +427,11 @@
         mean = joined(mean1, reduced)
         v = thin(mean, high_p[...], low_p[...]) * (2.0 / (count * penalty)) + answer[...]
         result = first + 2.0 * mean - thin(v, high_w[...], low_w[...])
+        primal1 = jnp.sum(jnp.square(first - mean), axis=0, keepdims=True)
         for k in range(owners):
-            own2[k] = result[:, k * wide : (k + 1) * wide]
-        scatter(own2, land2, send2, recv2)
+            own2[k, 0:reduced] = result[:, k * wide : (k + 1) * wide]
+            own2[k, reduced : reduced + 1] = primal1[:, k * wide : (k + 1) * wide]
+        scatter(own2, land2, send2, recv2, second_owners)
         change = (first - mean) + result
         for f in range(head):
             ship[f, 0] = result[f * half : (f + 1) * half]
@@ -407,27 +439,24 @@
             copy(ship.at[f], mine, ship_send.at[f], ship_recv, me, f).start()
         mine[0] = result[head * half :]
         mine[1] = change[head * half :]
-        pl.when(inside)(owner_second)
-
-        def sent(size):
-            departed(own1, size, send1)
-            departed(own2, size, send2)
-
-        split_on(inside, lambda: sent(owners - 1), lambda: sent(owners))
+        pl.when(inside2)(owner_second)
+
+        split_on(inside1, lambda: departed(own1, owners - 1, send1), lambda: departed(own1, owners, send1))
+        split_on(inside2, lambda: departed(own2, owners - 1, send2), lambda: departed(own2, owners, send2))
         for f in range(head):
             copy(ship.at[f], mine, ship_send.at[f], ship_recv, me, core).wait_send()
 
     def follower():
         split_on(
             inside,
-            lambda: pl.semaphore_wait(barrier, owners),
-            lambda: pl.semaphore_wait(barrier, owners + 1),
+            lambda: pl.semaphore_wait(barrier, len(everyones)),
+            lambda: pl.semaphore_wait(barrier, len(everyones) + 1),
         )
         copy(ship.at[0], mine, ship_send.at[0], ship_recv, me, core).wait_recv()
 
     split_on(leading, leader, follower)
     split_on(
-        leading & inside,
+        leading & inside2,
         lambda: arrived(mean2, owners - 1, got2),
         lambda: arrived(mean2, owners, got2),
     )
@@ -441,9 +470,12 @@
     sums = jnp.sum(sums, axis=1, keepdims=True)
     history[...] = jnp.broadcast_to(jnp.sqrt(sums * (1.0 / (slabs * reduced * width))), history.shape)
 
-    @pl.when(leading & inside)
+    @pl.when(leading & inside1)
     def _():
         departed(land1, slabs - 1, spread1)
+
+    @pl.when(leading & inside2)
+    def _():
         departed(span, slabs * feats - 1, spread2)
 
 
@@ -457,7 +489,7 @@
         out_history[r : r + 1, :] = jnp.concatenate([history[2 * r + k : 2 * r + k + 1, 0:1] for k in range(2)], 1)
 
 
-def shards(states, inputs, targets):
+def shards(states, inputs, targets, *, spots):
     reduced, own = states.shape
     feats = lax.axis_size("feat")
     slabs = lax.axis_size("slab")
@@ -487,23 +519,29 @@
         ],
         compiler_params=pltpu.CompilerParams(vmem_limit_bytes=LIMIT, collective_id=1, has_side_effects=True),
         name="exchange",
-    )(states, inputs[None], targets)
+    )(*[pltpu.with_memory_space_constraint(x, pltpu.HBM) for x in (states, inputs[None], targets)])
     square = shape(count, count)
     short = shape(count, count, dtype=BF16)
     solved = pl.pallas_call(
         inverse_kernel,
-        out_shape=(short, short, square, short, short),
+        out_shape=(short, short, square, shape(1, LANES)),
         in_specs=[vmem] * 2,
-        out_specs=(vmem,) * 5,
-        scratch_shapes=[hold(count, count), hold(count, count, dtype=BF16)],
+        out_specs=(vmem,) * 4,
+        scratch_shapes=[
+            hold(count, count), hold(count, count, dtype=BF16),
+            hold(count, count, dtype=BF16), hold(count, count, dtype=BF16),
+        ],
         compiler_params=pltpu.CompilerParams(vmem_limit_bytes=LIMIT),
         name="local_inverse",
     )(gathered[0], gathered[1])
     block = shape(half, columns)
+    first_owners, second_owners, order = choose(spots, owners)
     after, duals, last, history = pl.pallas_call(
-        functools.partial(second_kernel, width=width),
+        functools.partial(
+            second_kernel, width=width, first_owners=first_owners, second_owners=second_owners, order=order
+        ),
         out_shape=(block, block, block, shape(4, LANES)),
-        in_specs=[vmem] * 8,
+        in_specs=[vmem] * 7,
         out_specs=(vmem,) * 4,
         scratch_shapes=[
             hold(columns, count),
@@ -511,8 +549,8 @@
             hold(count, columns, dtype=BF16), hold(count, columns, dtype=BF16),
             hold(count, count), hold(count, count, dtype=BF16), hold(count, count, dtype=BF16),
             hold(count, count, dtype=BF16), hold(reduced, count),
-            hold(owners, reduced, wide), hold(owners, reduced, wide),
-            hold(slabs, reduced, wide), hold(slabs, reduced, wide),
+            hold(owners, reduced, wide), hold(owners, reduced + 1, wide),
+            hold(slabs, reduced, wide), hold(slabs, reduced + 1, wide),
             hold(reduced, wide), hold(feats, half + 4, wide),
             hold(owners, reduced, wide), hold(owners, half + 4, wide),
             hold(2, half, columns), hold(max(feats - 1, 1), 2, half, columns),
@@ -535,7 +573,19 @@
     return (jnp.swapaxes(after, 0, 1), jnp.swapaxes(duals, 0, 1), last, history)
 
 
+def choose(spots, owners):
+    slabs = range(len(spots))
+    apart = [[sum(abs(a - b) for a, b in zip(spots[p], spots[q])) for q in slabs] for p in slabs]
+    first = sorted(slabs, key=lambda q: (max(apart[q]), -apart[0][q], q))[:owners]
+    second = sorted(slabs, key=lambda q: (max(apart[q]), apart[0][q], q))[:owners]
+    return sorted(first), sorted(second), sorted(slabs, key=lambda p: (apart[0][p], p))
+
+
 def solution(mesh):
+    spots = [
+        tuple(getattr(device, "coords", None) or (index,)) for index, device in enumerate(mesh.devices[:, 0])
+    ]
     in_specs = (P(None, ("slab", "feat")), P(("slab", "feat")), P(None, ("slab", "feat")))
     out_specs = (P("slab", "feat", None), P("slab", "feat", None), P("feat", None), P())
-    return jax.shard_map(shards, mesh=mesh, in_specs=in_specs, out_specs=out_specs, check_vma=False)
+    body = functools.partial(shards, spots=spots)
+    return jax.shard_map(body, mesh=mesh, in_specs=in_specs, out_specs=out_specs, check_vma=False)

time: 35.9 us -> 32.7 us (0.911)
  local copies, waits for them, and re-layouts: 2.23 us -> 0 us
  Pallas kernels: 32.7 us -> 31.9 us
    unnamed x6 -> x0, local copies, waits for them, and re-layouts: 2.23 us -> none
    pallas_call x2, Pallas kernels: 30.4 us -> 29.4 us  [the longest x1 29.3 us: shards(): pl.pallas_call(functools.partial(second_kernel, width=width, first_owners...]
where the time goes in v3:
time: 32.7 us; the launch traced here: 32.5 us
  Pallas kernels  31.9 us (98%)
  between operations  0.65 us (2%)
    pallas_call x1, Pallas kernels, shards(): pl.pallas_call(functools.partial(second_kernel, width=width, first_owners...  29.3 us
    pallas_call x1, Pallas kernels, shards(): pl.pallas_call(exchange_kernel, out_shape=(shape(reduced, count), shape(1...  1.83 us
    pallas_call x1, Pallas kernels, shards(): pl.pallas_call(last_kernel, out_shape=(spread_rows, spread_rows, shard, s...  0.71 us

profile of v3, /device:TPU:0, one launch (start us, length us, event | category | flops | bytes accessed | tf_op | source)
XLA Modules:
  0.0 32.5 jit_solution(6762790227301876217)
XLA Ops:
  0.6 1.8 %exchange.1 = (f32[40,512]{1,0:T(8,128)S(1)}, f32[1,512]{1,0:T(1,128)S(1)}, f32[40,512]{1,0:T(8,128)S(1)}) custom-call(f32[40,256]{1,0:T(8,128)} %states.1, f32[1,256]{1,0:T(1,128)} %bitcast.3, f32[40,256]{1,0:T(8,128)} %targets.1), custom_call_target="tpu_custom_call" | custom-call | tf_op jit(solution)/shard_map/exchange/pallas_call | solution.py:512
  2.5 29.3 %second_and_averages.1 = (f32[20,896]{1,0:T(8,128)S(1)}, f32[20,896]{1,0:T(8,128)S(1)}, f32[20,896]{1,0:T(8,128)S(1)}, f32[4,128]{1,0:T(4,128)S(1)}) custom-call(f32[40,512]{1,0:T(8,128)S(1)} %get-tuple-element.19.all_s, f32[1,512]{1,0:T(1,128)S(1)} %get-tuple-element.20.all_u, f32[40,512]{1,0:T(8,128)S(1)} %get-tuple-element.21.all_t, ...), custom_call_target="tpu_custom_call" | custom-call | tf_op jit(solution)/shard_map/second_and_averages/pallas_call | solution.py:539
  31.8 0.7 %outputs.1 = (f32[20,1,862]{2,1,0:T(1,128)}, f32[20,1,862]{2,1,0:T(1,128)}, f32[20,862]{1,0:T(8,128)}, f32[2,2]{1,0:T(2,128)}) custom-call(f32[20,896]{1,0:T(8,128)S(1)} %get-tuple-element.26.after, f32[20,896]{1,0:T(8,128)S(1)} %get-tuple-element.27.duals, f32[20,896]{1,0:T(8,128)S(1)} %get-tuple-element.28.last, f32[4,128]{1,0:T(4,128)S(1)} %get-tuple-element.29.history), custom_call_target="tpu_custom_call" | custom-call | tf_op jit(solution)/shard_map/outputs/pallas_call | solution.py:565
  (1 shorter events, 0.0 us)

commit v4 on v3

--- a/solution.py
+++ b/solution.py
@@ -46,6 +46,14 @@
 
 def eye(size):
     return jnp.where(eye_mask(size), 1.0, 0.0)
+
+
+def less_eye(value, target, part):
+    for p in range(0, value.shape[0], LANES):
+        for q in range(part.start, part.stop, LANES):
+            piece = value[p : p + LANES, q - part.start : q - part.start + LANES]
+            piece = piece - eye(LANES) if p == q else piece
+            target[p : p + LANES, q : q + LANES] = piece.astype(BF16)
 
 
 def invert_by_pivots(source, target):
@@ -138,7 +146,7 @@
     return 2.0 / (2.0 - delta * delta), delta * delta / (2.0 - delta * delta)
 
 
-def inverse_kernel(all_s, all_u, high_a, low_a, inverse, info, system, shifted, high_x, low_x):
+def inverse_kernel(all_s, all_u, high_a, low_a, start, inverse, info, system, shifted, high_x, low_x):
     reduced, count = all_s.shape
     edge = LANES
     spans = [slice(k, k + edge) for k in range(0, count, edge)]
@@ -167,18 +175,23 @@
         delta = (high - 1.0) / (high + 1.0)
         alpha = 2.0 / ((1.0 + high) * penalty)
         c, later = newton_scale(delta)
-        for p, down in enumerate(spans):
-            for q, across in enumerate(spans):
-                part = (-c * alpha * alpha) * system[down, across]
-                if p == q:
-                    part = part + jnp.where(eye_mask(edge), 2.0 * c * alpha, 0.0)
-                inverse[down, across] = part
+
+        def begin(target, dtype):
+            for p, down in enumerate(spans):
+                for q, across in enumerate(spans):
+                    part = (-c * alpha * alpha) * system[down, across]
+                    if p == q:
+                        part = part + jnp.where(eye_mask(edge), 2.0 * c * alpha, 0.0)
+                    target[down, across] = part.astype(dtype)
+
+        begin(start, BF16)
         hard = jnp.logical_not(high <= EASY)
         lane = lax.broadcasted_iota(jnp.int32, (1, LANES), 1)
         info[...] = jnp.where(lane == 0, later, jnp.where(hard, 1.0, 0.0))
 
         @pl.when(hard)
         def _():
+            begin(inverse, F32)
             careful(later)
 
     def careful(delta):
@@ -218,17 +231,34 @@
     pl.when(lax.axis_index("feat") == lax.axis_size("feat") - 1)(solve)
 
 
-def build_features(all_s, all_u, phi):
+def feature_steps(all_s, all_u, phi, high_p, low_p):
     reduced, count = all_s.shape
+
+    def first():
+        phi[0:reduced, :] = all_s[...]
+
+    def products(i, row):
+        phi[row : row + reduced - i, :] = all_s[i : i + 1, :] * all_s[i:reduced, :]
+
+    def ending(row):
+        phi[row : row + 1, :] = all_u[...]
+        phi[row + 1 : row + 2, :] = jnp.ones((1, count), F32)
+        if row + 2 < phi.shape[0]:
+            phi[row + 2 :, :] = jnp.zeros((phi.shape[0] - row - 2, count), F32)
+
+    steps = [first]
     row = reduced
-    phi[0:reduced, :] = all_s[...]
     for i in range(reduced):
-        phi[row : row + reduced - i, :] = all_s[i : i + 1, :] * all_s[i:reduced, :]
+        steps.append(functools.partial(products, i, row))
         row += reduced - i
-    phi[row : row + 1, :] = all_u[...]
-    phi[row + 1 : row + 2, :] = jnp.ones((1, count), F32)
-    if row + 2 < phi.shape[0]:
-        phi[row + 2 :, :] = jnp.zeros((phi.shape[0] - row - 2, count), F32)
+    steps.append(functools.partial(ending, row))
+
+    def narrow(rows):
+        high_p[rows, :], low_p[rows, :] = split(phi[rows, :])
+
+    for k in range(0, phi.shape[0], LANES):
+        steps.append(functools.partial(narrow, slice(k, k + LANES)))
+    return steps
 
 
 def lanes_of(value):
@@ -236,7 +266,7 @@
 
 
 def second_kernel(
-    all_s, all_u, all_t, high_a, low_a, inverse, info, after, duals, last, history,
+    all_s, all_u, all_t, high_a, low_a, begin, inverse, info, after, duals, last, history,
     phi, high_p, low_p, high_w, low_w, better, high_b, low_b, gap, answer,
     own1, own2, land1, land2, out1, out2, mean1, mean2, mine, ship, span,
     send1, recv1, spread1, got1, send2, recv2, spread2, got2, ship_send, ship_recv,
@@ -372,23 +402,33 @@
         ah, al = high_a[...], low_a[...]
         delta = info[0:1, 0:1]
         kept = info[0:1, 1:2] > 0.5
-        better[...] = inverse[...]
-
-        def coarse(step, delta):
-            x = better[...].astype(BF16)
-            gap[...] = dot(high_a[...], x).astype(BF16)
-            c, later = newton_scale(delta)
-            value = better[...]
-            better[...] = jnp.where(kept, value, c * (2.0 * value - dot(x, gap[...])))
-            return later
-
-        lax.fori_loop(0, STEPS, coarse, delta)
+        middle = up(count // 2, LANES)
+        parts = (slice(0, middle), slice(middle, count))
+        steps = feature_steps(all_s, all_u, phi, high_p, low_p)
+        chunk = -(-len(steps) // (2 * STEPS))
+        old, fresh, spare = begin, high_b, low_b
+        size = jnp.ones((1, 1), F32)
+        for step in range(STEPS):
+            c, delta = newton_scale(delta)
+            for part in parts:
+                gap[:, part] = dot(ah, old[:, part]).astype(BF16)
+                for _ in range(min(chunk, len(steps))):
+                    steps.pop(0)()
+            x = old[...]
+            for part in parts:
+                value = (2.0 / size) * old[:, part].astype(F32) - dot(x, gap[:, part])
+                if step == STEPS - 1:
+                    value = value * (c * size * size)
+                fresh[:, part] = value.astype(BF16)
+            size = c * size * size
+            old, fresh, spare = fresh, spare, fresh
         b = all_t[...] * (1.0 / count)
-        build_features(all_s, all_u, phi)
-        high_p[...], low_p[...] = split(phi[...])
-        x = better[...].astype(BF16)
-        gap[...] = (eye(count) - (dot(ah, x) + dot(al, x))).astype(BF16)
-        better[...] = jnp.where(kept, better[...], x.astype(F32) + dot(x, gap[...]))
+        x = old[...]
+        for part in parts:
+            less_eye(dot(ah, x[:, part]) + dot(al, x[:, part]), gap, part)
+        for part in parts:
+            value = x[:, part].astype(F32) - dot(x, gap[:, part])
+            better[:, part] = jnp.where(kept, inverse[:, part], value)
         high_b[...], low_b[...] = split(better[...])
         xh, xl = high_b[...], low_b[...]
         y = thin(b, xh, xl)
@@ -405,13 +445,13 @@
         )
         scatter(own1, land1, send1, recv1, first_owners)
 
-        gap[...] = (eye(count) - (dot(ah, xh) + (dot(ah, xl) + dot(al, xh)))).astype(BF16)
-        better[...] = better[...] + dot(xh, gap[...])
-        high_b[...], low_b[...] = split(better[...])
-        bh, bl = high_b[...], low_b[...]
-        gap[...] = (eye(count) - (dot(ah, bh) + (dot(ah, bl) + dot(al, bh)))).astype(BF16)
-        better[...] = better[...] + dot(bh, gap[...])
-        high_b[...], low_b[...] = split(better[...])
+        for _ in range(2):
+            bh, bl = high_b[...], low_b[...]
+            for part in parts:
+                less_eye(dot(ah, bh[:, part]) + (dot(ah, bl[:, part]) + dot(al, bh[:, part])), gap, part)
+            for part in parts:
+                better[:, part] = better[:, part] - dot(bh, gap[:, part])
+            high_b[...], low_b[...] = split(better[...])
         pl.when(inside1)(owner_first)
         weights = dot(high_b[...], high_p[...], NT) + (
             dot(high_b[...], low_p[...], NT) + dot(low_b[...], high_p[...], NT)
@@ -524,9 +564,9 @@
     short = shape(count, count, dtype=BF16)
     solved = pl.pallas_call(
         inverse_kernel,
-        out_shape=(short, short, square, shape(1, LANES)),
+        out_shape=(short, short, short, square, shape(1, LANES)),
         in_specs=[vmem] * 2,
-        out_specs=(vmem,) * 4,
+        out_specs=(vmem,) * 5,
         scratch_shapes=[
             hold(count, count), hold(count, count, dtype=BF16),
             hold(count, count, dtype=BF16), hold(count, count, dtype=BF16),
@@ -541,7 +581,7 @@
             second_kernel, width=width, first_owners=first_owners, second_owners=second_owners, order=order
         ),
         out_shape=(block, block, block, shape(4, LANES)),
-        in_specs=[vmem] * 7,
+        in_specs=[vmem] * 8,
         out_specs=(vmem,) * 4,
         scratch_shapes=[
             hold(columns, count),

time: 32.7 us -> 31.5 us (0.963)
  Pallas kernels: 31.9 us -> 30.6 us
    pallas_call x1, Pallas kernels: 29.3 us -> 28.1 us  [shards(): pl.pallas_call(functools.partial(second_kernel, width=width, first_owners...]
where the time goes in v4:
time: 31.5 us; the launch traced here: 31.3 us
  Pallas kernels  30.6 us (97%)
  between operations  0.65 us (2%)
    pallas_call x1, Pallas kernels, shards(): pl.pallas_call(functools.partial(second_kernel, width=width, first_owners...  28.1 us
    pallas_call x1, Pallas kernels, shards(): pl.pallas_call(exchange_kernel, out_shape=(shape(reduced, count), shape(1...  1.83 us
    pallas_call x1, Pallas kernels, shards(): pl.pallas_call(last_kernel, out_shape=(spread_rows, spread_rows, shard, s...  0.71 us

profile of v4, /device:TPU:0, one launch (start us, length us, event | category | flops | bytes accessed | tf_op | source)
XLA Modules:
  0.0 31.3 jit_solution(6938048569492826115)
XLA Ops:
  0.6 1.8 %exchange.1 = (f32[40,512]{1,0:T(8,128)S(1)}, f32[1,512]{1,0:T(1,128)S(1)}, f32[40,512]{1,0:T(8,128)S(1)}) custom-call(f32[40,256]{1,0:T(8,128)} %states.1, f32[1,256]{1,0:T(1,128)} %bitcast.3, f32[40,256]{1,0:T(8,128)} %targets.1), custom_call_target="tpu_custom_call" | custom-call | tf_op jit(solution)/shard_map/exchange/pallas_call | solution.py:552
  2.5 28.1 %second_and_averages.1 = (f32[20,896]{1,0:T(8,128)S(1)}, f32[20,896]{1,0:T(8,128)S(1)}, f32[20,896]{1,0:T(8,128)S(1)}, f32[4,128]{1,0:T(4,128)S(1)}) custom-call(f32[40,512]{1,0:T(8,128)S(1)} %get-tuple-element.20.all_s, f32[1,512]{1,0:T(1,128)S(1)} %get-tuple-element.21.all_u, f32[40,512]{1,0:T(8,128)S(1)} %get-tuple-element.22.all_t, ...), custom_call_target="tpu_custom_call" | custom-call | tf_op jit(solution)/shard_map/second_and_averages/pallas_call | solution.py:579
  30.6 0.7 %outputs.1 = (f32[20,1,862]{2,1,0:T(1,128)}, f32[20,1,862]{2,1,0:T(1,128)}, f32[20,862]{1,0:T(8,128)}, f32[2,2]{1,0:T(2,128)}) custom-call(f32[20,896]{1,0:T(8,128)S(1)} %get-tuple-element.28.after, f32[20,896]{1,0:T(8,128)S(1)} %get-tuple-element.29.duals, f32[20,896]{1,0:T(8,128)S(1)} %get-tuple-element.30.last, f32[4,128]{1,0:T(4,128)S(1)} %get-tuple-element.31.history), custom_call_target="tpu_custom_call" | custom-call | tf_op jit(solution)/shard_map/outputs/pallas_call | solution.py:605
  (1 shorter events, 0.0 us)

commit v5 on v4

--- a/solution.py
+++ b/solution.py
@@ -77,23 +77,21 @@
     lax.fori_loop(0, size, step, 0)
 
 
-def exchange_kernel(
-    states, inputs, targets, all_s, all_u, all_t, near_s, near_u, near_t, local, send, recv
-):
+def exchange_kernel(states, inputs, targets, all_s, all_u, all_t, local, send, recv):
     feats = lax.axis_size("feat")
     core = lax.axis_index("feat")
     head = feats - 1
     own = states.shape[1]
     sources = (states, inputs, targets)
-    nears = (near_s, near_u, near_t)
     alls = (all_s, all_u, all_t)
 
-    def load(i, target):
-        return pltpu.make_async_copy(sources[i], target, local.at[i])
+    def load(i):
+        return pltpu.make_async_copy(sources[i], alls[i].at[:, pl.ds(head * own, own)], local.at[i])
 
     def move(i, f):
         return pltpu.make_async_remote_copy(
-            src_ref=nears[i], dst_ref=alls[i].at[:, pl.ds(f * own, own)], send_sem=send.at[i], recv_sem=recv.at[f, i],
+            src_ref=sources[i], dst_ref=alls[i].at[:, pl.ds(f * own, own)],
+            send_sem=send.at[i], recv_sem=recv.at[f, i],
             device_id={"feat": head}, device_id_type=pl.DeviceIdType.MESH,
         )
 
@@ -104,13 +102,13 @@
 
     @pl.when(core == head)
     def _():
-        for i in range(3):
-            load(i, alls[i].at[:, pl.ds(head * own, own)]).start()
         for f in range(head):
             greet(f)
+        for i in range(3):
+            load(i).start()
         pl.semaphore_wait(barrier, head)
         for i in range(3):
-            load(i, alls[i].at[:, pl.ds(head * own, own)]).wait()
+            load(i).wait()
         for f in range(head):
             for i in range(3):
                 move(i, f).wait_recv()
@@ -119,12 +117,9 @@
 
         @pl.when(core == f)
         def _():
-            for i in range(3):
-                load(i, nears[i]).start()
             greet(head)
             pl.semaphore_wait(barrier, 1)
             for i in range(3):
-                load(i, nears[i]).wait()
                 move(i, f).start()
             for i in range(3):
                 move(i, f).wait_send()
@@ -355,8 +350,10 @@
     def _():
         greet(me, head)
 
-    def scatter(source, landing, send, recv, slab_list):
+    def scatter(source, landing, send, recv, slab_list, group):
         for k, slab in enumerate(slab_list):
+            if k not in group:
+                continue
 
             @pl.when(me != slab)
             def _():
@@ -397,6 +394,9 @@
         for slab in order:
             one(slab)
         mean2[spot2] = out2[head]
+
+    near_half = -(-owners // 2)
+    groups = (range(0, near_half), range(near_half, owners))
 
     def leader():
         ah, al = high_a[...], low_a[...]
@@ -435,15 +435,19 @@
         y = y + thin(b - thin(y, ah, al), xh, xl)
         y = y + thin(b - thin(y, ah, al), xh, xl)
         answer[...] = y
-        start_value = thin(y, high_p[...], low_p[...], NT)
-        for k in range(owners):
-            own1[k] = start_value[:, k * wide : (k + 1) * wide]
-        split_on(
-            inside,
-            lambda: pl.semaphore_wait(barrier, slabs * feats - 1),
-            lambda: pl.semaphore_wait(barrier, len(everyones) + feats - 1),
-        )
-        scatter(own1, land1, send1, recv1, first_owners)
+        for group in groups:
+            across = slice(group.start * wide, group.stop * wide)
+            start_value = thin(y, high_p[across, :], low_p[across, :], NT)
+            for k in group:
+                near = (k - group.start) * wide
+                own1[k] = start_value[:, near : near + wide]
+            if group is groups[0]:
+                split_on(
+                    inside,
+                    lambda: pl.semaphore_wait(barrier, slabs * feats - 1),
+                    lambda: pl.semaphore_wait(barrier, len(everyones) + feats - 1),
+                )
+            scatter(own1, land1, send1, recv1, first_owners, group)
 
         for _ in range(2):
             bh, bl = high_b[...], low_b[...]
@@ -466,12 +470,18 @@
         first = joined(own1, reduced)
         mean = joined(mean1, reduced)
         v = thin(mean, high_p[...], low_p[...]) * (2.0 / (count * penalty)) + answer[...]
-        result = first + 2.0 * mean - thin(v, high_w[...], low_w[...])
         primal1 = jnp.sum(jnp.square(first - mean), axis=0, keepdims=True)
-        for k in range(owners):
-            own2[k, 0:reduced] = result[:, k * wide : (k + 1) * wide]
-            own2[k, reduced : reduced + 1] = primal1[:, k * wide : (k + 1) * wide]
-        scatter(own2, land2, send2, recv2, second_owners)
+        results = []
+        for group in groups:
+            across = slice(group.start * wide, group.stop * wide)
+            result = first[:, across] + 2.0 * mean[:, across] - thin(v, high_w[:, across], low_w[:, across])
+            for k in group:
+                near = (k - group.start) * wide
+                own2[k, 0:reduced] = result[:, near : near + wide]
+                own2[k, reduced : reduced + 1] = primal1[:, k * wide : (k + 1) * wide]
+            scatter(own2, land2, send2, recv2, second_owners, group)
+            results.append(result)
+        result = jnp.concatenate(results, 1)
         change = (first - mean) + result
         for f in range(head):
             ship[f, 0] = result[f * half : (f + 1) * half]
@@ -554,9 +564,7 @@
         out_shape=(shape(reduced, count), shape(1, count), shape(reduced, count)),
         in_specs=[pl.BlockSpec(memory_space=pltpu.HBM)] * 3,
         out_specs=(vmem,) * 3,
-        scratch_shapes=[
-            hold(reduced, own), hold(1, own), hold(reduced, own), dma((3,)), dma((3,)), dma((feats, 3)),
-        ],
+        scratch_shapes=[dma((3,)), dma((3,)), dma((feats, 3))],
         compiler_params=pltpu.CompilerParams(vmem_limit_bytes=LIMIT, collective_id=1, has_side_effects=True),
         name="exchange",
     )(*[pltpu.with_memory_space_constraint(x, pltpu.HBM) for x in (states, inputs[None], targets)])

time: 31.5 us -> 30.5 us (0.968)
  Pallas kernels: 30.6 us -> 29.7 us
    pallas_call x1, Pallas kernels: 28.1 us -> 27.2 us  [shards(): pl.pallas_call(functools.partial(second_kernel, width=width, first_owners...]
where the time goes in v5:
time: 30.5 us; the launch traced here: 30.4 us
  Pallas kernels  29.7 us (97%)
  between operations  0.65 us (2%)
    pallas_call x1, Pallas kernels, shards(): pl.pallas_call(functools.partial(second_kernel, width=width, first_owners...  27.2 us
    pallas_call x1, Pallas kernels, shards(): pl.pallas_call(exchange_kernel, out_shape=(shape(reduced, count), shape(1...  1.75 us
    pallas_call x1, Pallas kernels, shards(): pl.pallas_call(last_kernel, out_shape=(spread_rows, spread_rows, shard, s...  0.71 us

profile of v5, /device:TPU:0, one launch (start us, length us, event | category | flops | bytes accessed | tf_op | source)
XLA Modules:
  0.0 30.4 jit_solution(12966141370379343614)
XLA Ops:
  0.6 1.8 %exchange.1 = (f32[40,512]{1,0:T(8,128)S(1)}, f32[1,512]{1,0:T(1,128)S(1)}, f32[40,512]{1,0:T(8,128)S(1)}) custom-call(f32[40,256]{1,0:T(8,128)} %states.1, f32[1,256]{1,0:T(1,128)} %bitcast.3, f32[40,256]{1,0:T(8,128)} %targets.1), custom_call_target="tpu_custom_call" | custom-call | tf_op jit(solution)/shard_map/exchange/pallas_call | solution.py:562
  2.4 27.2 %second_and_averages.1 = (f32[20,896]{1,0:T(8,128)S(1)}, f32[20,896]{1,0:T(8,128)S(1)}, f32[20,896]{1,0:T(8,128)S(1)}, f32[4,128]{1,0:T(4,128)S(1)}) custom-call(f32[40,512]{1,0:T(8,128)S(1)} %get-tuple-element.20.all_s, f32[1,512]{1,0:T(1,128)S(1)} %get-tuple-element.21.all_u, f32[40,512]{1,0:T(8,128)S(1)} %get-tuple-element.22.all_t, ...), custom_call_target="tpu_custom_call" | custom-call | tf_op jit(solution)/shard_map/second_and_averages/pallas_call | solution.py:587
  29.7 0.7 %outputs.1 = (f32[20,1,862]{2,1,0:T(1,128)}, f32[20,1,862]{2,1,0:T(1,128)}, f32[20,862]{1,0:T(8,128)}, f32[2,2]{1,0:T(2,128)}) custom-call(f32[20,896]{1,0:T(8,128)S(1)} %get-tuple-element.28.after, f32[20,896]{1,0:T(8,128)S(1)} %get-tuple-element.29.duals, f32[20,896]{1,0:T(8,128)S(1)} %get-tuple-element.30.last, f32[4,128]{1,0:T(4,128)S(1)} %get-tuple-element.31.history), custom_call_target="tpu_custom_call" | custom-call | tf_op jit(solution)/shard_map/outputs/pallas_call | solution.py:613
  (1 shorter events, 0.0 us)

commit v6 on v5

--- a/solution.py
+++ b/solution.py
@@ -10,8 +10,8 @@
 penalty = 1.0
 LIMIT = 20 * 2**20
 LANES = 128
-STEPS = 4
-EASY = 400.0
+STEPS = 3
+EASY = 200.0
 NN = (((1,), (0,)), ((), ()))
 NT = (((1,), (1,)), ((), ()))
 TN = (((0,), (0,)), ((), ()))
@@ -164,9 +164,12 @@
                     part = part + jnp.where(eye_mask(edge), penalty, 0.0)
                 system[down, across] = part
                 high_a[down, across], low_a[down, across] = split(part)
-                sums[q] = sums[q] + jnp.abs(part).reshape(edge // 8, 8, edge).sum(0)
-        sums = functools.reduce(jnp.maximum, [jnp.sum(part, axis=0, keepdims=True) for part in sums])
-        high = jnp.max(sums) / penalty
+                size = jnp.abs(part)
+                shifted[down, across] = size.astype(BF16)
+                sums[q] = sums[q] + size.reshape(edge // 8, 8, edge).sum(0)
+        sums = jnp.concatenate([jnp.broadcast_to(jnp.sum(part, axis=0, keepdims=True), (8, edge)) for part in sums], 1)
+        trial = sums.astype(BF16)
+        high = jnp.max(dot(trial, shifted[...]) / trial.astype(F32)) * (1.005 / penalty)
         delta = (high - 1.0) / (high + 1.0)
         alpha = 2.0 / ((1.0 + high) * penalty)
         c, later = newton_scale(delta)
@@ -426,8 +429,9 @@
         x = old[...]
         for part in parts:
             less_eye(dot(ah, x[:, part]) + dot(al, x[:, part]), gap, part)
+        c, _ = newton_scale(delta)
         for part in parts:
-            value = x[:, part].astype(F32) - dot(x, gap[:, part])
+            value = c * (x[:, part].astype(F32) - dot(x, gap[:, part]))
             better[:, part] = jnp.where(kept, inverse[:, part], value)
         high_b[...], low_b[...] = split(better[...])
         xh, xl = high_b[...], low_b[...]

time: 30.5 us -> 30.1 us (0.987)
  Pallas kernels: 29.7 us -> 29.3 us
    pallas_call x1, Pallas kernels: 27.2 us -> 26.8 us  [shards(): pl.pallas_call(functools.partial(second_kernel, width=width, first_owners...]
where the time goes in v6:
time: 30.1 us; the launch traced here: 29.9 us
  Pallas kernels  29.3 us (97%)
  between operations  0.65 us (2%)
    pallas_call x1, Pallas kernels, shards(): pl.pallas_call(functools.partial(second_kernel, width=width, first_owners...  26.8 us
    pallas_call x1, Pallas kernels, shards(): pl.pallas_call(exchange_kernel, out_shape=(shape(reduced, count), shape(1...  1.75 us
    pallas_call x1, Pallas kernels, shards(): pl.pallas_call(last_kernel, out_shape=(spread_rows, spread_rows, shard, s...  0.71 us

profile of v6, /device:TPU:0, one launch (start us, length us, event | category | flops | bytes accessed | tf_op | source)
XLA Modules:
  0.0 29.9 jit_solution(15567086363277448654)
XLA Ops:
  0.6 1.8 %exchange.1 = (f32[40,512]{1,0:T(8,128)S(1)}, f32[1,512]{1,0:T(1,128)S(1)}, f32[40,512]{1,0:T(8,128)S(1)}) custom-call(f32[40,256]{1,0:T(8,128)} %states.1, f32[1,256]{1,0:T(1,128)} %bitcast.3, f32[40,256]{1,0:T(8,128)} %targets.1), custom_call_target="tpu_custom_call" | custom-call | tf_op jit(solution)/shard_map/exchange/pallas_call | solution.py:566
  2.4 26.8 %second_and_averages.1 = (f32[20,896]{1,0:T(8,128)S(1)}, f32[20,896]{1,0:T(8,128)S(1)}, f32[20,896]{1,0:T(8,128)S(1)}, f32[4,128]{1,0:T(4,128)S(1)}) custom-call(f32[40,512]{1,0:T(8,128)S(1)} %get-tuple-element.20.all_s, f32[1,512]{1,0:T(1,128)S(1)} %get-tuple-element.21.all_u, f32[40,512]{1,0:T(8,128)S(1)} %get-tuple-element.22.all_t, ...), custom_call_target="tpu_custom_call" | custom-call | tf_op jit(solution)/shard_map/second_and_averages/pallas_call | solution.py:591
  29.2 0.7 %outputs.1 = (f32[20,1,862]{2,1,0:T(1,128)}, f32[20,1,862]{2,1,0:T(1,128)}, f32[20,862]{1,0:T(8,128)}, f32[2,2]{1,0:T(2,128)}) custom-call(f32[20,896]{1,0:T(8,128)S(1)} %get-tuple-element.28.after, f32[20,896]{1,0:T(8,128)S(1)} %get-tuple-element.29.duals, f32[20,896]{1,0:T(8,128)S(1)} %get-tuple-element.30.last, f32[4,128]{1,0:T(4,128)S(1)} %get-tuple-element.31.history), custom_call_target="tpu_custom_call" | custom-call | tf_op jit(solution)/shard_map/outputs/pallas_call | solution.py:617
  (1 shorter events, 0.0 us)

commit v7 on v6

--- a/solution.py
+++ b/solution.py
@@ -398,8 +398,8 @@
             one(slab)
         mean2[spot2] = out2[head]
 
-    near_half = -(-owners // 2)
-    groups = (range(0, near_half), range(near_half, owners))
+    near_half = -(-owners // 3)
+    groups = [range(k, min(k + near_half, owners)) for k in range(0, owners, near_half)]
 
     def leader():
         ah, al = high_a[...], low_a[...]

time: 30.1 us -> 30 us (level)
  no operation moved by 1% of the time
where the time goes in v7:
time: 30 us; the launch traced here: 29.9 us
  Pallas kernels  29.2 us (97%)
  between operations  0.65 us (2%)
    pallas_call x1, Pallas kernels, shards(): pl.pallas_call(functools.partial(second_kernel, width=width, first_owners...  26.7 us
    pallas_call x1, Pallas kernels, shards(): pl.pallas_call(exchange_kernel, out_shape=(shape(reduced, count), shape(1...  1.75 us
    pallas_call x1, Pallas kernels, shards(): pl.pallas_call(last_kernel, out_shape=(spread_rows, spread_rows, shard, s...  0.71 us

profile of v7, /device:TPU:0, one launch (start us, length us, event | category | flops | bytes accessed | tf_op | source)
XLA Modules:
  0.0 29.9 jit_solution(2727572098520340211)
XLA Ops:
  0.6 1.8 %exchange.1 = (f32[40,512]{1,0:T(8,128)S(1)}, f32[1,512]{1,0:T(1,128)S(1)}, f32[40,512]{1,0:T(8,128)S(1)}) custom-call(f32[40,256]{1,0:T(8,128)} %states.1, f32[1,256]{1,0:T(1,128)} %bitcast.3, f32[40,256]{1,0:T(8,128)} %targets.1), custom_call_target="tpu_custom_call" | custom-call | tf_op jit(solution)/shard_map/exchange/pallas_call | solution.py:566
  2.4 26.7 %second_and_averages.1 = (f32[20,896]{1,0:T(8,128)S(1)}, f32[20,896]{1,0:T(8,128)S(1)}, f32[20,896]{1,0:T(8,128)S(1)}, f32[4,128]{1,0:T(4,128)S(1)}) custom-call(f32[40,512]{1,0:T(8,128)S(1)} %get-tuple-element.20.all_s, f32[1,512]{1,0:T(1,128)S(1)} %get-tuple-element.21.all_u, f32[40,512]{1,0:T(8,128)S(1)} %get-tuple-element.22.all_t, ...), custom_call_target="tpu_custom_call" | custom-call | tf_op jit(solution)/shard_map/second_and_averages/pallas_call | solution.py:591
  29.2 0.7 %outputs.1 = (f32[20,1,862]{2,1,0:T(1,128)}, f32[20,1,862]{2,1,0:T(1,128)}, f32[20,862]{1,0:T(8,128)}, f32[2,2]{1,0:T(2,128)}) custom-call(f32[20,896]{1,0:T(8,128)S(1)} %get-tuple-element.28.after, f32[20,896]{1,0:T(8,128)S(1)} %get-tuple-element.29.duals, f32[20,896]{1,0:T(8,128)S(1)} %get-tuple-element.30.last, f32[4,128]{1,0:T(4,128)S(1)} %get-tuple-element.31.history), custom_call_target="tpu_custom_call" | custom-call | tf_op jit(solution)/shard_map/outputs/pallas_call | solution.py:617
  (1 shorter events, 0.0 us)

commit v8 on v7

--- a/solution.py
+++ b/solution.py
@@ -630,7 +630,7 @@
     apart = [[sum(abs(a - b) for a, b in zip(spots[p], spots[q])) for q in slabs] for p in slabs]
     first = sorted(slabs, key=lambda q: (max(apart[q]), -apart[0][q], q))[:owners]
     second = sorted(slabs, key=lambda q: (max(apart[q]), apart[0][q], q))[:owners]
-    return sorted(first), sorted(second), sorted(slabs, key=lambda p: (apart[0][p], p))
+    return sorted(first), sorted(second, reverse=True), sorted(slabs, key=lambda p: (apart[0][p], p))
 
 
 def solution(mesh):

time: 30 us -> 29.9 us (level)
  no operation moved by 1% of the time
where the time goes in v8:
time: 29.9 us; the launch traced here: 29.8 us
  Pallas kernels  29.1 us (97%)
  between operations  0.65 us (2%)
    pallas_call x1, Pallas kernels, shards(): pl.pallas_call(functools.partial(second_kernel, width=width, first_owners...  26.6 us
    pallas_call x1, Pallas kernels, shards(): pl.pallas_call(exchange_kernel, out_shape=(shape(reduced, count), shape(1...  1.75 us
    pallas_call x1, Pallas kernels, shards(): pl.pallas_call(last_kernel, out_shape=(spread_rows, spread_rows, shard, s...  0.71 us

profile of v8, /device:TPU:0, one launch (start us, length us, event | category | flops | bytes accessed | tf_op | source)
XLA Modules:
  0.0 29.8 jit_solution(16948976696525279933)
XLA Ops:
  0.6 1.8 %exchange.1 = (f32[40,512]{1,0:T(8,128)S(1)}, f32[1,512]{1,0:T(1,128)S(1)}, f32[40,512]{1,0:T(8,128)S(1)}) custom-call(f32[40,256]{1,0:T(8,128)} %states.1, f32[1,256]{1,0:T(1,128)} %bitcast.3, f32[40,256]{1,0:T(8,128)} %targets.1), custom_call_target="tpu_custom_call" | custom-call | tf_op jit(solution)/shard_map/exchange/pallas_call | solution.py:566
  2.4 26.6 %second_and_averages.1 = (f32[20,896]{1,0:T(8,128)S(1)}, f32[20,896]{1,0:T(8,128)S(1)}, f32[20,896]{1,0:T(8,128)S(1)}, f32[4,128]{1,0:T(4,128)S(1)}) custom-call(f32[40,512]{1,0:T(8,128)S(1)} %get-tuple-element.20.all_s, f32[1,512]{1,0:T(1,128)S(1)} %get-tuple-element.21.all_u, f32[40,512]{1,0:T(8,128)S(1)} %get-tuple-element.22.all_t, ...), custom_call_target="tpu_custom_call" | custom-call | tf_op jit(solution)/shard_map/second_and_averages/pallas_call | solution.py:591
  29.0 0.7 %outputs.1 = (f32[20,1,862]{2,1,0:T(1,128)}, f32[20,1,862]{2,1,0:T(1,128)}, f32[20,862]{1,0:T(8,128)}, f32[2,2]{1,0:T(2,128)}) custom-call(f32[20,896]{1,0:T(8,128)S(1)} %get-tuple-element.28.after, f32[20,896]{1,0:T(8,128)S(1)} %get-tuple-element.29.duals, f32[20,896]{1,0:T(8,128)S(1)} %get-tuple-element.30.last, f32[4,128]{1,0:T(4,128)S(1)} %get-tuple-element.31.history), custom_call_target="tpu_custom_call" | custom-call | tf_op jit(solution)/shard_map/outputs/pallas_call | solution.py:617
  (1 shorter events, 0.0 us)
